TPU v7x, 128 devices: a whole 4x4x4 slice. The times are simulated.
128 devices in a mesh: row: 8 (over y_hi, x), col: 16 (over y_lo, z, core).
Axes of the slice: x: 4, y: 4 (y_hi: 2, y_lo: 2; y = y_hi * 2 + y_lo), z: 4, core: 2. Of those that a mesh axis runs over, the one named last changes fastest.
Arguments:
- front_matrix: float32 [8, 8, 256, 4, 16, 256], P(None, 'row', None, None, 'col'), may hold values from -6 to 6
- swap_rows: int32 [3, 256], replicated, may hold values from 0 to 16383, as said below
- l_inverse: float32 [3, 256, 256], replicated, may hold values from -1 to 1, as said below
- u_inverse: float32 [3, 256, 256], replicated, may hold values from -1 to 1, as said below
- contrib_tiles: float32 [12288, 128, 128], P(('row', 'col')), may hold values from -6 to 6
- tile_owner: int32 [12288, 1], P(('row', 'col')), may hold values from 0 to 127; in each aligned block of 96 rows (0 to 95, 96 to 191, ...) at most 2 rows name the same one
- tile_spot: int32 [12288], P(('row', 'col')), may hold values from 0 to 127
Outputs:
- factored: float32 [8, 8, 256, 4, 16, 256], P(None, 'row', None, None, 'col')
Inputs may be any that keep to these rules, and one draw needn't show every extreme that they name: For every k and j, swap_rows[k, j] is either k * 256 + j or a row of (k + 1) * 256 or more; within one k the entries of the second kind are distinct. Each l_inverse[k] is unit lower triangular. Each u_inverse[k] is upper triangular with a positive diagonal. `tile_owner`: among the 96 tiles held by one device, at most 2 have the same owner; some device's tiles reach that bound.
All inputs are finite; a program needn't handle non-finite values.
Results may differ from a plain program's by a relative error of at most 0.00015.
Values sent between devices are 32-bit elements; how exact they have to be, the bound alone decides.
No kernel may reach another device: no remote copies, remote signals or barrier semaphores. Data moves between devices by JAX's collectives and lax.ppermute only.
A program may use at most 192 MiB of HBM per device.

v0:
```python
import jax
import jax.numpy as jnp
from jax import lax
from jax.experimental import pallas as pl
from jax.experimental.pallas import tpu as pltpu
from jax.sharding import PartitionSpec as P


STEPS = 3
CAP = 2
NB = 256
LANES = 128
GROUPS = 8
RING = 16
PARCEL = 48
F32 = jnp.float32
BF16 = jnp.bfloat16
I32 = jnp.int32
ANY = pl.BlockSpec(memory_space=pl.ANY)
SMEM = pl.BlockSpec(memory_space=pltpu.SMEM)
BIG = pltpu.CompilerParams(vmem_limit_bytes=60 * 1024 * 1024)


def halves(x):
    high = x.astype(BF16)
    return high, (x - high.astype(F32)).astype(BF16)


def product(a, b):
    def one(x, y):
        return jnp.dot(x, y, preferred_element_type=F32)

    return one(a[0], b[0]) + (one(a[0], b[1]) + one(a[1], b[0]))


def pack_body(owner, spot, tiles, *rest):
    send, ids, held, seen, load_sem, sem = rest[-6:]
    count = tiles.shape[0]
    load = pltpu.make_async_copy(tiles, held, load_sem)
    load.start()

    def clear(i, carry):
        ids[i] = -1
        return carry

    def fresh(i, carry):
        seen[i] = 0
        return carry

    lax.fori_loop(0, ids.shape[0], clear, 0)
    lax.fori_loop(0, seen.shape[0], fresh, 0)
    load.wait()

    def put(i, carry):
        d = owner[i]
        rank = seen[d]
        seen[d] = rank + 1
        slot = d * CAP + rank
        ids[slot] = spot[i]
        pltpu.make_async_copy(held.at[i], send.at[slot], sem).start()
        return carry

    lax.fori_loop(0, count, put, 0)
    pltpu.make_async_copy(held, send.at[pl.ds(0, count)], sem).wait()


def pack(tiles, owner, spot, devices):
    edge = tiles.shape[1]
    return pl.pallas_call(
        pack_body,
        in_specs=[SMEM, SMEM, ANY],
        out_specs=[ANY, SMEM],
        out_shape=[
            jax.ShapeDtypeStruct((devices * CAP, edge, edge), F32),
            jax.ShapeDtypeStruct((devices * CAP,), I32),
        ],
        scratch_shapes=[
            pltpu.VMEM(tiles.shape, F32),
            pltpu.SMEM((devices,), I32),
            pltpu.SemaphoreType.DMA(()),
            pltpu.SemaphoreType.DMA(()),
        ],
        compiler_params=BIG,
        name="pack_tiles",
    )(owner, spot, tiles)


def pick_body(me, place, rows, *rest):
    outs, corner, held, sem = rest[:-3], rest[-3], rest[-2], rest[-1]
    held[...] = jnp.zeros_like(held)

    def go(i, n):
        at = place[i]

        @pl.when(at >= 0)
        def _():
            pltpu.make_async_copy(rows.at[at], held.at[i], sem).start()

        return n + (at >= 0).astype(I32)

    started = lax.fori_loop(0, place.shape[0], go, 0)

    def finish(i, carry):
        pltpu.make_async_copy(rows.at[0], held.at[0], sem).wait()
        return carry

    lax.fori_loop(0, started, finish, 0)
    for g in range(2):
        corner[:, g * LANES : (g + 1) * LANES] = held[:, g, :]
    for t, out in enumerate(outs):
        share = out.shape[0]
        out[...] = held[pl.ds(lax.rem(me[0] + t, len(outs)) * share, share)]


def pick(me, place, rows, count):
    total = place.shape[0]
    vmem = pl.BlockSpec(memory_space=pltpu.VMEM)
    return pl.pallas_call(
        pick_body,
        in_specs=[SMEM, SMEM, ANY],
        out_specs=[vmem] * (count + 1),
        out_shape=[jax.ShapeDtypeStruct((total // count, GROUPS, LANES), F32)] * count
        + [jax.ShapeDtypeStruct((total, NB), F32)],
        scratch_shapes=[pltpu.VMEM((total, GROUPS, LANES), F32), pltpu.SemaphoreType.DMA(())],
        compiler_params=BIG,
        name="pick_rows",
    )(me, place, rows)


def collect_body(*refs):
    total = refs[0][...]
    for ref in refs[1:-1]:
        total = total + ref[...]
    refs[-1][...] = total


def collect(given):
    vmem = pl.BlockSpec(memory_space=pltpu.VMEM)
    return pl.pallas_call(
        collect_body,
        in_specs=[vmem] * len(given),
        out_specs=vmem,
        out_shape=jax.ShapeDtypeStruct(given[0].shape, F32),
        compiler_params=BIG,
        name="collect_rows",
    )(*given)


def parcel_body(turn, row, rows, *rest):
    outs, seen, sem = rest[:-2], rest[-2], rest[-1]
    for t in range(len(outs)):
        seen[t] = 0

    def go(i, n):
        to = turn[i]
        at = seen[jnp.maximum(to, 0)]
        fits = (to >= 0) & (at < PARCEL)

        @pl.when(fits)
        def _():
            seen[to] = at + 1
            for t, out in enumerate(outs):

                @pl.when(to == t)
                def _():
                    pltpu.make_async_copy(rows.at[row[i]], out.at[at], sem).start()

        return n + fits.astype(I32)

    started = lax.fori_loop(0, turn.shape[0], go, 0)

    def finish(i, carry):
        pltpu.make_async_copy(rows.at[0], outs[0].at[0], sem).wait()
        return carry

    lax.fori_loop(0, started, finish, 0)


def parcel(turn, row, rows, count):
    vmem = pl.BlockSpec(memory_space=pltpu.VMEM)
    return pl.pallas_call(
        parcel_body,
        in_specs=[SMEM, SMEM, ANY],
        out_specs=[vmem] * count,
        out_shape=[jax.ShapeDtypeStruct((PARCEL, GROUPS, LANES), F32)] * count,
        scratch_shapes=[pltpu.SMEM((count,), I32), pltpu.SemaphoreType.DMA(())],
        compiler_params=BIG,
        name="parcel_rows",
    )(turn, row, rows)


def land_body(ranked, turn, row, was, rows, corner, notes, *rest):
    parcels = rest[:-8]
    out, parts, stack, seen, at_row, at_turn, at_rank, total = rest[-8:]
    step = pl.program_id(0)
    tall = rows.shape[0]
    height = tall // 2
    share = corner.shape[0] // 2

    @pl.when(step == 0)
    def _():
        for t, given in enumerate(parcels):
            seen[t] = 0
            stack[t] = given[...]

        def note(i, n):
            to = turn[i]

            @pl.when(to >= 0)
            def _():
                at_row[n] = row[i]
                at_turn[n] = to
                rank = seen[to]
                seen[to] = rank + 1
                at_rank[n] = jnp.minimum(rank, PARCEL - 1) if ranked else was[i]

            return n + (to >= 0).astype(I32)

        total[0] = lax.fori_loop(0, turn.shape[0], note, 0)

    out[...] = rows[...]
    first = step * tall

    def settle(i, carry):
        at = at_row[i] - first

        @pl.when((at >= 0) & (at < tall))
        def _():
            out[at] = stack[at_turn[i], at_rank[i]]

        return carry

    lax.fori_loop(0, total[0], settle, 0)
    for s in range(2):
        for g in range(2):
            parts[s, :height, g * LANES : (g + 1) * LANES] = out[s * height : (s + 1) * height, g, :]
        parts[s, height : height + share] = corner[s * share : (s + 1) * share]
        parts[s, height + share :] = notes[s]


def land_rows(turn, row, was, rows, corner, notes, parcels, ranked):
    count = notes.shape[0]
    tall = rows.shape[0] // count * 2
    share = corner.shape[0] // count
    slab = pl.BlockSpec((tall, GROUPS, LANES), lambda i: (i, 0, 0))
    events = turn.shape[0]
    length = tall // 2 + share + notes.shape[1]

    def body(*refs):
        return land_body(ranked, *refs)

    return pl.pallas_call(
        body,
        grid=(count // 2,),
        in_specs=[
            SMEM,
            SMEM,
            SMEM,
            slab,
            pl.BlockSpec((2 * share, NB), lambda i: (i, 0)),
            pl.BlockSpec((2,) + notes.shape[1:], lambda i: (i, 0, 0)),
        ]
        + [pl.BlockSpec(p.shape, lambda i: (0, 0, 0)) for p in parcels],
        out_specs=[slab, pl.BlockSpec((2, length, NB), lambda i: (i, 0, 0))],
        out_shape=[
            jax.ShapeDtypeStruct(rows.shape, F32),
            jax.ShapeDtypeStruct((count, length, NB), F32),
        ],
        scratch_shapes=[
            pltpu.VMEM((len(parcels),) + parcels[0].shape, F32),
            pltpu.SMEM((len(parcels),), I32),
            pltpu.SMEM((events,), I32),
            pltpu.SMEM((events,), I32),
            pltpu.SMEM((events,), I32),
            pltpu.SMEM((1,), I32),
        ],
        compiler_params=BIG,
        name="land_ranked" if ranked else "land_whole",
    )(turn, row, was, rows, corner, notes, *parcels)


def main_body(me, linv, uinv, gathered, panels, block, *rest):
    chunks = rest[:-9]
    out, chosen, final, upper, upper_hi, upper_lo, factor, corner, sem = rest[-9:]
    step = pl.program_id(0)
    height = panels.shape[2]

    def ui(k):
        return halves(uinv[k])

    @pl.when(step == 0)
    def _():
        copy = pltpu.make_async_copy(gathered.at[:, :, pl.ds(height, corner.shape[2]), :], corner, sem)
        copy.start()
        for t, chunk in enumerate(chunks):
            share = chunk.shape[0]
            chosen[pl.ds(lax.rem(me[0] - t + len(chunks), len(chunks)) * share, share)] = chunk[...]
        copy.wait()
        cols = [corner[:, k].reshape(STEPS * NB, NB) for k in range(STEPS)]
        n = [[cols[k][i * NB : (i + 1) * NB] for k in range(STEPS)] for i in range(STEPS)]
        low = {}
        for k in range(STEPS):
            x = chosen[k * NB : (k + 1) * NB].reshape(NB, GROUPS * LANES)
            for m in range(k):
                x = x - product(low[k, m], (upper_hi[m * NB : (m + 1) * NB], upper_lo[m * NB : (m + 1) * NB]))
            u = product(halves(linv[k]), halves(x))
            hi, lo = halves(u)
            upper[k * NB : (k + 1) * NB] = u
            upper_hi[k * NB : (k + 1) * NB] = hi
            upper_lo[k * NB : (k + 1) * NB] = lo
            final[k, k] = n[k][k]
            for i in range(k + 1, STEPS):
                l = product(halves(n[i][k]), ui(k))
                low[i, k] = halves(l)
                final[i, k] = l
                v = product(halves(linv[k]), halves(n[k][i]))
                final[k, i] = v
            for i in range(k + 1, STEPS):
                for j in range(k + 1, STEPS):
                    n[i][j] = n[i][j] - product(low[i, k], halves(final[k, j]))

    hi = []
    lo = []
    for k in range(STEPS):
        x = panels[:, k].reshape(2 * height, NB)
        for m in range(k):
            x = x - product((hi[m], lo[m]), halves(final[m, k]))
        l = product(halves(x), ui(k))
        factor[k] = l
        h, w = halves(l)
        hi.append(h)
        lo.append(w)
    high = jnp.concatenate(hi, axis=1)
    rest = jnp.concatenate(lo, axis=1)
    update = product((high, rest), (upper_hi[...], upper_lo[...]))
    value = block[...].reshape(2 * height, GROUPS * LANES) - update
    for s in range(2):
        for g in range(GROUPS):
            out[s, g] = value[s * height : (s + 1) * height, g * LANES : (g + 1) * LANES]

    @pl.when(me[1] < STEPS)
    def _():
        for s in range(2):
            for g in range(2):
                out[s, g] = factor[me[1], s * height : (s + 1) * height, g * LANES : (g + 1) * LANES]

    is_top = (step == 0) & (me[0] < STEPS)

    @pl.when(is_top)
    def _():
        base = me[0] * NB
        for s in range(2):
            u = upper[pl.ds(base + s * height, height), :]
            for g in range(GROUPS):
                out[s, g] = u[:, g * LANES : (g + 1) * LANES]

    @pl.when(is_top & (me[1] < STEPS))
    def _():
        for s in range(2):
            for g in range(2):
                out[s, g] = final[me[0], me[1], s * height : (s + 1) * height, g * LANES : (g + 1) * LANES]


def eliminate(me, linv, uinv, gathered, rows, chunks):
    parts, _, both, _ = gathered.shape
    height = rows.shape[0] // parts
    share = both - height
    width = GROUPS * LANES
    whole3 = pl.BlockSpec((STEPS, NB, NB), lambda i: (0, 0, 0))
    return pl.pallas_call(
        main_body,
        grid=(parts // 2,),
        in_specs=[
            SMEM,
            whole3,
            whole3,
            ANY,
            pl.BlockSpec((2, STEPS, height, NB), lambda i: (i, 0, 0, 0)),
            pl.BlockSpec((2 * height, GROUPS, LANES), lambda i: (i, 0, 0)),
        ]
        + [pl.BlockSpec(c.shape, lambda i: (0, 0, 0)) for c in chunks],
        out_specs=pl.BlockSpec((2, GROUPS, height, LANES), lambda i: (i, 0, 0, 0)),
        out_shape=jax.ShapeDtypeStruct((parts, GROUPS, height, LANES), F32),
        scratch_shapes=[
            pltpu.VMEM((STEPS * NB, GROUPS, LANES), F32),
            pltpu.VMEM((STEPS, STEPS, NB, NB), F32),
            pltpu.VMEM((STEPS * NB, width), F32),
            pltpu.VMEM((STEPS * NB, width), BF16),
            pltpu.VMEM((STEPS * NB, width), BF16),
            pltpu.VMEM((STEPS, NB, NB), F32),
            pltpu.VMEM((parts, STEPS, share, NB), F32),
            pltpu.SemaphoreType.DMA(()),
        ],
        compiler_params=BIG,
        name="eliminate",
    )(me, linv, uinv, gathered, gathered, rows, *chunks)


def tail_body(ids, base, received, out, acc, ring, staged, order, base_sem, ring_sem, out_sem):
    whole = pltpu.make_async_copy(base, acc, base_sem)
    whole.start()
    edge = acc.shape[1]

    def note(i, n):
        order[n] = i
        return n + (ids[i] >= 0).astype(I32)

    total = lax.fori_loop(0, ids.shape[0], note, 0)

    def fetch(j):
        b = lax.rem(j, RING)
        return pltpu.make_async_copy(received.at[order[j]], ring.at[b], ring_sem.at[b])

    def prime(j, carry):
        fetch(j).start()
        return carry

    lax.fori_loop(0, jnp.minimum(total, RING), prime, 0)
    whole.wait()

    def add(j, carry):
        fetch(j).wait()
        m = ids[order[j]]
        acc[m] = acc[m] + ring[lax.rem(j, RING)]

        @pl.when(j + RING < total)
        def _():
            fetch(j + RING).start()

        return carry

    lax.fori_loop(0, total, add, 0)
    copies = []
    for s in range(acc.shape[0] // GROUPS):
        p = s % 2
        if s >= 2:
            copies[s - 2].wait()
        for g in range(GROUPS):
            staged[p, :, g, :] = acc[s * GROUPS + g]
        copy = pltpu.make_async_copy(staged.at[p], out.at[pl.ds(s * edge, edge)], out_sem.at[p])
        copy.start()
        copies.append(copy)
    copies[-2].wait()
    copies[-1].wait()


def add_tiles(ids, base, received):
    spots, edge, _ = base.shape
    return pl.pallas_call(
        tail_body,
        in_specs=[SMEM, ANY, ANY],
        out_specs=ANY,
        out_shape=jax.ShapeDtypeStruct((spots // GROUPS * edge, GROUPS, LANES), F32),
        scratch_shapes=[
            pltpu.VMEM((spots, edge, LANES), F32),
            pltpu.VMEM((RING, edge, LANES), F32),
            pltpu.VMEM((2, edge, GROUPS, LANES), F32),
            pltpu.SMEM((ids.shape[0],), I32),
            pltpu.SemaphoreType.DMA(()),
            pltpu.SemaphoreType.DMA((RING,)),
            pltpu.SemaphoreType.DMA((2,)),
        ],
        compiler_params=BIG,
        name="add_tiles",
    )(ids, base, received)


def look(x, t, values, other):
    same = x[:, None] == t[None, :]
    hit = jnp.any(same, axis=1)
    return hit, jnp.where(hit, jnp.sum(jnp.where(same, values[None, :], 0), axis=1), other)


def permutation(swap_rows):
    t0, t1, t2 = swap_rows[0], swap_rows[1], swap_rows[2]
    j = jnp.arange(NB, dtype=I32)
    n = NB
    x = jnp.concatenate([NB + j, 2 * NB + j, t1, t2])
    _, once = look(x, t0, j, x)
    v1 = once[:n]
    y = jnp.concatenate([2 * NB + j, t2])
    _, twice = look(y, t1, v1, jnp.concatenate([once[n : 2 * n], once[3 * n :]]))
    v2 = twice[:n]
    source = jnp.concatenate([t0, once[2 * n : 3 * n], twice[n:]])
    below = STEPS * NB
    in1 = jnp.any(t0[:, None] == t1[None, :], axis=1)
    in2 = jnp.any(jnp.concatenate([t0, t1])[:, None] == t2[None, :], axis=1)
    ok0 = (t0 >= below) & ~in1 & ~in2[:n]
    ok1 = (t1 >= below) & ~in2[n:]
    ok2 = t2 >= below
    land = jnp.where(jnp.concatenate([ok0, ok1, ok2]), jnp.concatenate([t0, t1, t2]), -1)
    return source, land, jnp.concatenate([j, v1, v2])


def step(front_matrix, swap_rows, l_inverse, u_inverse, contrib_tiles, tile_owner, tile_spot):
    row_count = lax.axis_size("row")
    col_count = lax.axis_size("col")
    row_place = lax.axis_index("row").astype(I32)
    col_place = lax.axis_index("col").astype(I32)
    me = jnp.stack([row_place, col_place])
    local_rows = front_matrix.shape[0] * NB
    rows = front_matrix.reshape(-1).reshape(local_rows, GROUPS, LANES)

    def exchange(x, axes):
        return lax.all_to_all(x, axes, split_axis=0, concat_axis=0, tiled=True)

    def shift(x, t):
        return lax.ppermute(x, "row", [(p, (p + t) % row_count) for p in range(row_count)])

    def leave(x, t):
        return lax.ppermute(x, "row", [(p, (p + t) % row_count) for p in range(STEPS)])

    def home(x):
        block = x // NB
        here = (x >= 0) & (block % row_count == row_place)
        return jnp.where(here, block // row_count * NB + x % NB, -1)

    source, land, old = permutation(swap_rows)
    from_row = old // NB
    to_row = land // NB % row_count
    going = jnp.where((land >= 0) & (from_row == row_place), (to_row - row_place) % row_count, -1)
    coming = jnp.where((land >= 0) & (to_row == row_place), (row_place - from_row) % row_count, -1)
    pair = jnp.where(land >= 0, from_row * row_count + to_row, -1)
    loads = jnp.sum((pair[:, None] == jnp.arange(STEPS * row_count, dtype=I32)[None, :]).astype(I32), axis=0)

    parcels = parcel(going, old % NB, rows, row_count)
    parcels = [parcels[0]] + [leave(parcels[t], t) for t in range(1, row_count)]
    picked = pick(me, home(source), rows, row_count)
    picked, corner = list(picked[:-1]), picked[-1]
    given = [picked[0]] + [shift(picked[t], t) for t in range(1, row_count)]
    send, ids = pack(contrib_tiles, tile_owner[:, 0], tile_spot, row_count * col_count)
    notes = ids.astype(F32).reshape(row_count, col_count, CAP).transpose(1, 0, 2).reshape(col_count, -1)
    notes = jnp.pad(notes[:, None, :], ((0, 0), (0, 7), (0, NB - notes.shape[1])))

    def ranked(parcels):
        return land_rows(coming, home(land), old % NB, rows, corner, notes, parcels, True)

    def whole(parcels):
        every = [rows[:NB]] + [leave(rows[:NB], t) for t in range(1, row_count)]
        return land_rows(coming, home(land), old % NB, rows, corner, notes, every, False)

    moved, parts = lax.cond(jnp.max(loads) > PARCEL, whole, ranked, parcels)
    dealt = exchange(parts, "col")
    tall = local_rows // col_count
    partial = dealt[:STEPS, tall:-8].reshape(-1, NB)
    notes = dealt[:, -8, : row_count * CAP].reshape(col_count, row_count, CAP).transpose(1, 0, 2)
    notes = jnp.pad(notes.reshape(1, -1), ((0, 7), (0, NB - notes.size)))
    partial = jnp.concatenate([partial, notes])
    partial = jnp.stack([partial] + [shift(partial, t) for t in range(1, row_count)])
    corner = jnp.sum(partial[:, :-8], axis=0).reshape(STEPS, -1, NB)
    mixed = jnp.concatenate([dealt[:STEPS, :tall], corner], axis=1)
    gathered = lax.all_gather(mixed.reshape(-1, NB), "col", axis=0, tiled=True)
    gathered = gathered.reshape(col_count, STEPS, -1, NB)
    notes = partial[:, -8].reshape(row_count, -1)[:, : row_count * col_count * CAP]
    notes = lax.dynamic_slice_in_dim(notes, row_place * col_count * CAP, col_count * CAP, 1)
    turn = (row_place - jnp.arange(row_count, dtype=I32)) % row_count
    ids_in = notes[turn].reshape(-1).astype(I32)
    summed = collect(given)
    chunks = [summed] + [shift(summed, t) for t in range(1, row_count)]
    send, gathered, *chunks = lax.optimization_barrier((send, gathered, *chunks))
    received = exchange(send, ("row", "col"))
    base = eliminate(me, l_inverse, u_inverse, gathered, moved, chunks)
    out = add_tiles(ids_in, base.reshape(-1, LANES, LANES), received)
    return out.reshape(-1).reshape(front_matrix.shape)


def solution(mesh):
    placed = (
        P(None, "row", None, None, "col", None),
        P(),
        P(),
        P(),
        P(("row", "col"), None, None),
        P(("row", "col"), None),
        P(("row", "col")),
    )
    return jax.shard_map(
        step,
        mesh=mesh,
        in_specs=placed,
        out_specs=P(None, "row", None, None, "col", None),
        check_vma=False,
    )
```

profile of v0, /device:TPU:12, one launch (start us, length us, event | category | flops | bytes accessed | tf_op | source)
XLA Modules:
  0.0 580.3 jit_solution(18381892392979884572)
XLA Ops:
  10.3 35.7 %parcel_rows.1 = (f32[48,8,128]{2,1,0:T(8,128)S(1)}, f32[48,8,128]{2,1,0:T(8,128)}, f32[48,8,128]{2,1,0:T(8,128)}, f32[48,8,128]{2,1,0:T(8,128)}, f32[48,8,128]{...) custom-call(s32[768]{0:T(1024)} %get-tuple-element.199.turn, ...), custom_call_target="tpu_custom_call" | custom-call | tf_op jit(solution)/shard_map/parcel_rows/pallas_call | solution.py:181
  55.5 3.8 collective-permute-start.12
  62.4 6.7 %pack_tiles.1 = (f32[256,128,128]{2,1,0:T(8,128)}, s32[256]{0:T(256)}) custom-call(s32[96]{0:T(128)} %bitcast.72, s32[96]{0:T(128)} %spot.1, f32[96,128,128]{2,1,0:T(8,128)} %tiles.1), custom_call_target="tpu_custom_call" | custom-call | tf_op jit(solution)/shard_map/pack_tiles/pallas_call | solution.py:69
  70.7 9.2 %pick_rows.1 = (f32[96,8,128]{2,1,0:T(8,128)}, f32[96,8,128]{2,1,0:T(8,128)}, f32[96,8,128]{2,1,0:T(8,128)}, f32[96,8,128]{2,1,0:T(8,128)}, f32[96,8,128]{2,1,0:...) custom-call(s32[2]{0:T(128)} %pad_add_fusion.6.me, ...), custom_call_target="tpu_custom_call" | custom-call | tf_op jit(solution)/shard_map/pick_rows/pallas_call | solution.py:118
  80.0 25.2 %conditional.1 = ((f32[2048,8,128]{2,1,0:T(8,128)}, f32[16,184,256]{2,1,0:T(8,128)})) conditional(s32[]{:T(128)} %convert_element_type.19, (s32[768]{0:T(1024)S(1)}, s32[]{:T(128)}, s32[768]{0:T(1024)S(1)}, s32[768]{0:T(1024)S(1)}, f32[2048,8,128]{2,1,0:T(8,128)}, /*index=5*/f32[768,256]{1,0:T(8,128)S(1)}, f32[16,8,256]{0,2,1:T(8,128)S(1)}, ...), branch_computations={%region_8.9_spmd, %region_9.10_spmd} | conditional | flops 42240 | bytes 44315000 | solution.py:542
  81.6 23.6 %land_ranked.1 = (f32[2048,8,128]{2,1,0:T(8,128)}, f32[16,184,256]{2,1,0:T(8,128)}) custom-call(s32[768]{0:T(1024)S(1)} %get-tuple-element.49.refs_0_, s32[768]{0:T(1024)} %get-tuple-element.203.refs_1_, s32[768]{0:T(1024)} %get-tuple-element.202.refs_2_, f32[2048,8,128]{2,1,0:T(8,128)} %get-tuple-element.53.refs_3_, ...), custom_call_target="tpu_custom_call" | custom-call | tf_op jit(solution)/shard_map/cond/branch_0_fun/land_ranked/pallas_call | solution.py:252
  105.2 42.9 %all_to_all.10 = f32[16,184,256]{2,1,0:T(8,128)S(1)} all-to-all(f32[16,184,256]{2,1,0:T(8,128)} %get-tuple-element.112), channel_id=1, replica_groups=mesh['row'=8,'col'=16] {'col'}, dimensions={0} | all-to-all | bytes 6029312 | tf_op jit(solution)/shard_map/all_to_all | solution.py:505
  148.8 6.0 %collective-permute-start.15 = (f32[152,256]{1,0:T(8,128)S(1)}, f32[152,256]{1,0:T(8,128)S(1)}, u32[]{:S(2)}, u32[]{:S(2)}) collective-permute-start(f32[152,256]{1,0:T(8,128)S(1)} %select_maximum_fusion), channel_id=1, source_target_pairs={{0,32},{16,48},{32,64},{48,80},{64,96},{80,112},{96,0},{112,16},{1... | collective-permute-start | bytes 466952 | tf_op jit(solution)/shard_map/ppermute | solution.py:508
  154.8 5.5 collective-permute-start.17
  160.4 3.5 collective-permute-start.19
  164.1 7.8 %collective-permute-done.17 = f32[152,256]{1,0:T(8,128)S(1)} collective-permute-done((f32[152,256]{1,0:T(8,128)S(1)}, f32[152,256]{1,0:T(8,128)S(1)}, u32[]{:S(2)}, u32[]{:S(2)}) %collective-permute-start.17) | collective-permute-done | bytes 155680 | tf_op jit(solution)/shard_map/ppermute | solution.py:508
  179.7 4.3 collective-permute-start.24
  184.0 10.2 %collective-permute-done.21.refs_1_ = f32[96,8,128]{2,1,0:T(8,128)S(1)} collective-permute-done((f32[96,8,128]{2,1,0:T(8,128)S(1)}, f32[96,8,128]{2,1,0:T(8,128)S(1)}, u32[]{:S(2)}, u32[]{:S(2)}) %collective-permute-start.21) | collective-permute-done | bytes 393248 | tf_op jit(solution)/shard_map/ppermute | solution.py:508
  197.0 11.2 %collective-permute-done.23.refs_3_ = f32[96,8,128]{2,1,0:T(8,128)S(1)} collective-permute-done((f32[96,8,128]{2,1,0:T(8,128)}, f32[96,8,128]{2,1,0:T(8,128)S(1)}, u32[]{:S(2)}, u32[]{:S(2)}) %collective-permute-start.23) | collective-permute-done | bytes 393248 | tf_op jit(solution)/shard_map/ppermute | solution.py:508
  208.2 15.6 %collective-permute-done.24.refs_4_ = f32[96,8,128]{2,1,0:T(8,128)S(1)} collective-permute-done((f32[96,8,128]{2,1,0:T(8,128)}, f32[96,8,128]{2,1,0:T(8,128)S(1)}, u32[]{:S(2)}, u32[]{:S(2)}) %collective-permute-start.24) | collective-permute-done | bytes 393248 | tf_op jit(solution)/shard_map/ppermute | solution.py:508
  227.9 2.8 collective-permute-start.29
  234.1 3.9 collective-permute-start.32
  239.0 17.3 %collective-permute-start.33 = (f32[96,8,128]{2,1,0:T(8,128)}, f32[96,8,128]{2,1,0:T(8,128)}, u32[]{:S(2)}, u32[]{:S(2)}) collective-permute-start(f32[96,8,128]{2,1,0:T(8,128)} %collect_rows.1.rest_0_), channel_id=1, source_target_pairs={{0,96},{16,112},{32,0},{48,16},{64,32},{80,48},{96,64},{112,80},{1... | collective-permute-start | bytes 1179656 | tf_op jit(solution)/shard_map/ppermute | solution.py:508
  256.4 22.5 %collective-permute-done.31.rest_4_ = f32[96,8,128]{2,1,0:T(8,128)S(1)} collective-permute-done((f32[96,8,128]{2,1,0:T(8,128)}, f32[96,8,128]{2,1,0:T(8,128)S(1)}, u32[]{:S(2)}, u32[]{:S(2)}) %collective-permute-start.31) | collective-permute-done | bytes 393248 | tf_op jit(solution)/shard_map/ppermute | solution.py:508
  278.9 14.8 %all-gather.2.cloned.1.call-done = f32[8448,256]{1,0:T(8,128)} async-done(((f32[528,256]{1,0:T(8,128)}), f32[8448,256]{1,0:T(8,128)}) %all-gather.2.cloned.1.call-update) | async-done | bytes 8650768 | tf_op jit(solution)/shard_map/all_gather | solution.py:552
  293.7 6.6 %all-to-all-start.1 = ((f32[256,128,128]{2,1,0:T(8,128)}), f32[256,128,128]{2,1,0:T(8,128)}, u32[]{:S(2)}, u32[]{:S(2)}) async-start(f32[256,128,128]{2,1,0:T(8,128)} %get-tuple-element.132), calls=%async_computation.1 | async-start | bytes 33554432 | tf_op jit(solution)/shard_map/all_to_all | solution.py:505
  301.6 32.4 %eliminate.1 = f32[16,8,128,128]{3,2,1,0:T(8,128)} custom-call(s32[2]{0:T(128)} %pad_add_fusion.6.me, f32[3,256,256]{2,1,0:T(8,128)} %linv.1, f32[3,256,256]{2,1,0:T(8,128)} %uinv.1, f32[16,3,176,256]{3,2,1,0:T(8,128)} %bitcast.41, f32[16,3,176,256]{3,2,1,0:T(8,128)} %bitcast.42, f32[2048,8,128]{2,1,0:T(8,128)} %get-tuple-element.123.block, ...), custom_call_target="tpu_custom_call" | custom-call | tf_op jit(solution)/shard_map/eliminate/pallas_call | solution.py:370
  334.0 212.0 %all-to-all-done.1.received = f32[256,128,128]{2,1,0:T(8,128)} async-done(((f32[256,128,128]{2,1,0:T(8,128)}), f32[256,128,128]{2,1,0:T(8,128)}, u32[]{:S(2)}, u32[]{:S(2)}) %all-to-all-start.1) | async-done | bytes 16777248 | tf_op jit(solution)/shard_map/all_to_all | solution.py:505
  546.0 27.4 %add_tiles.1 = f32[2048,8,128]{2,1,0:T(8,128)} custom-call(s32[256]{0:T(256)} %convert_element_type.22.ids, f32[128,128,128]{2,1,0:T(8,128)} %bitcast.43, f32[256,128,128]{2,1,0:T(8,128)} %all-to-all-done.1.received), custom_call_target="tpu_custom_call" | custom-call | tf_op jit(solution)/shard_map/add_tiles/pallas_call | solution.py:449
  (122 shorter events, 39.9 us)
Async XLA Ops:
  6.5 287.1 %all-gather.2.cloned.1.call-start = ((), (), s32[]{:S(2)}) async-start(), calls=%async_computation.2 | async-start | bytes 9191424 | tf_op jit(solution)/shard_map/all_gather | solution.py:552
  49.9 30.0 %collective-permute-start.9 = (f32[48,8,128]{2,1,0:T(8,128)}, f32[48,8,128]{2,1,0:T(8,128)S(1)}, u32[]{:S(2)}, u32[]{:S(2)}) collective-permute-start(f32[48,8,128]{2,1,0:T(8,128)} %get-tuple-element.107), channel_id=1, source_target_pairs={{0,48},{16,64},{32,80},{1,49},{17,65},{33,81},{2,50},{18,66},{34,8... | collective-permute-start | bytes 589832 | tf_op jit(solution)/shard_map/ppermute | solution.py:511
  51.3 28.7 %collective-permute-start.10 = (f32[48,8,128]{2,1,0:T(8,128)}, f32[48,8,128]{2,1,0:T(8,128)S(1)}, u32[]{:S(2)}, u32[]{:S(2)}) collective-permute-start(f32[48,8,128]{2,1,0:T(8,128)} %get-tuple-element.108), channel_id=1, source_target_pairs={{0,64},{16,80},{32,96},{1,65},{17,81},{33,97},{2,66},{18,82},{34,9... | collective-permute-start | bytes 589832 | tf_op jit(solution)/shard_map/ppermute | solution.py:511
  52.6 27.4 %collective-permute-start.11 = (f32[48,8,128]{2,1,0:T(8,128)}, f32[48,8,128]{2,1,0:T(8,128)S(1)}, u32[]{:S(2)}, u32[]{:S(2)}) collective-permute-start(f32[48,8,128]{2,1,0:T(8,128)} %get-tuple-element.109), channel_id=1, source_target_pairs={{0,80},{16,96},{32,112},{1,81},{17,97},{33,113},{2,82},{18,98},{34... | collective-permute-start | bytes 589832 | tf_op jit(solution)/shard_map/ppermute | solution.py:511
  55.5 24.5 %collective-permute-start.12 = (f32[48,8,128]{2,1,0:T(8,128)}, f32[48,8,128]{2,1,0:T(8,128)S(1)}, u32[]{:S(2)}, u32[]{:S(2)}) collective-permute-start(f32[48,8,128]{2,1,0:T(8,128)} %get-tuple-element.110), channel_id=1, source_target_pairs={{0,96},{16,112},{32,0},{1,97},{17,113},{33,1},{2,98},{18,114},{34,... | collective-permute-start | bytes 589832 | tf_op jit(solution)/shard_map/ppermute | solution.py:511
  59.6 20.4 %collective-permute-start.13 = (f32[48,8,128]{2,1,0:T(8,128)}, f32[48,8,128]{2,1,0:T(8,128)S(1)}, u32[]{:S(2)}, u32[]{:S(2)}) collective-permute-start(f32[48,8,128]{2,1,0:T(8,128)} %get-tuple-element.111), channel_id=1, source_target_pairs={{0,112},{16,0},{32,16},{1,113},{17,1},{33,17},{2,114},{18,2},{34,1... | collective-permute-start | bytes 589832 | tf_op jit(solution)/shard_map/ppermute | solution.py:511
  148.5 11.9 %collective-permute-start.14 = (f32[152,256]{1,0:T(8,128)S(1)}, f32[152,256]{1,0:T(8,128)S(1)}, u32[]{:S(2)}, u32[]{:S(2)}) collective-permute-start(f32[152,256]{1,0:T(8,128)S(1)} %select_maximum_fusion), channel_id=1, source_target_pairs={{0,16},{16,32},{32,48},{48,64},{64,80},{80,96},{96,112},{112,0},{1... | collective-permute-start | bytes 466952 | tf_op jit(solution)/shard_map/ppermute | solution.py:508
  148.8 15.1 %collective-permute-start.15 = (f32[152,256]{1,0:T(8,128)S(1)}, f32[152,256]{1,0:T(8,128)S(1)}, u32[]{:S(2)}, u32[]{:S(2)}) collective-permute-start(f32[152,256]{1,0:T(8,128)S(1)} %select_maximum_fusion), channel_id=1, source_target_pairs={{0,32},{16,48},{32,64},{48,80},{64,96},{80,112},{96,0},{112,16},{1... | collective-permute-start | bytes 466952 | tf_op jit(solution)/shard_map/ppermute | solution.py:508
  154.8 17.1 %collective-permute-start.17 = (f32[152,256]{1,0:T(8,128)S(1)}, f32[152,256]{1,0:T(8,128)S(1)}, u32[]{:S(2)}, u32[]{:S(2)}) collective-permute-start(f32[152,256]{1,0:T(8,128)S(1)} %select_maximum_fusion), channel_id=1, source_target_pairs={{0,64},{16,80},{32,96},{48,112},{64,0},{80,16},{96,32},{112,48},{1... | collective-permute-start | bytes 466952 | tf_op jit(solution)/shard_map/ppermute | solution.py:508
  160.4 13.4 %collective-permute-start.19 = (f32[152,256]{1,0:T(8,128)S(1)}, f32[152,256]{1,0:T(8,128)S(1)}, u32[]{:S(2)}, u32[]{:S(2)}) collective-permute-start(f32[152,256]{1,0:T(8,128)S(1)} %select_maximum_fusion), channel_id=1, source_target_pairs={{0,96},{16,112},{32,0},{48,16},{64,32},{80,48},{96,64},{112,80},{1... | collective-permute-start | bytes 466952 | tf_op jit(solution)/shard_map/ppermute | solution.py:508
  174.9 19.4 %collective-permute-start.21 = (f32[96,8,128]{2,1,0:T(8,128)S(1)}, f32[96,8,128]{2,1,0:T(8,128)S(1)}, u32[]{:S(2)}, u32[]{:S(2)}) collective-permute-start(f32[96,8,128]{2,1,0:T(8,128)S(1)} %copy-done.14), channel_id=1, source_target_pairs={{0,16},{16,32},{32,48},{48,64},{64,80},{80,96},{96,112},{112,0},{1... | collective-permute-start | bytes 1179656 | tf_op jit(solution)/shard_map/ppermute | solution.py:508
  177.3 19.7 %collective-permute-start.22 = (f32[96,8,128]{2,1,0:T(8,128)}, f32[96,8,128]{2,1,0:T(8,128)S(1)}, u32[]{:S(2)}, u32[]{:S(2)}) collective-permute-start(f32[96,8,128]{2,1,0:T(8,128)} %get-tuple-element.116), channel_id=1, source_target_pairs={{0,32},{16,48},{32,64},{48,80},{64,96},{80,112},{96,0},{112,16},{1... | collective-permute-start | bytes 1179656 | tf_op jit(solution)/shard_map/ppermute | solution.py:508
  178.5 29.7 %collective-permute-start.23 = (f32[96,8,128]{2,1,0:T(8,128)}, f32[96,8,128]{2,1,0:T(8,128)S(1)}, u32[]{:S(2)}, u32[]{:S(2)}) collective-permute-start(f32[96,8,128]{2,1,0:T(8,128)} %get-tuple-element.117), channel_id=1, source_target_pairs={{0,48},{16,64},{32,80},{48,96},{64,112},{80,0},{96,16},{112,32},{1... | collective-permute-start | bytes 1179656 | tf_op jit(solution)/shard_map/ppermute | solution.py:508
  179.7 44.1 %collective-permute-start.24 = (f32[96,8,128]{2,1,0:T(8,128)}, f32[96,8,128]{2,1,0:T(8,128)S(1)}, u32[]{:S(2)}, u32[]{:S(2)}) collective-permute-start(f32[96,8,128]{2,1,0:T(8,128)} %get-tuple-element.118), channel_id=1, source_target_pairs={{0,64},{16,80},{32,96},{48,112},{64,0},{80,16},{96,32},{112,48},{1... | collective-permute-start | bytes 1179656 | tf_op jit(solution)/shard_map/ppermute | solution.py:508
  184.0 39.8 %collective-permute-start.25 = (f32[96,8,128]{2,1,0:T(8,128)}, f32[96,8,128]{2,1,0:T(8,128)S(1)}, u32[]{:S(2)}, u32[]{:S(2)}) collective-permute-start(f32[96,8,128]{2,1,0:T(8,128)} %get-tuple-element.119), channel_id=1, source_target_pairs={{0,80},{16,96},{32,112},{48,0},{64,16},{80,32},{96,48},{112,64},{1... | collective-permute-start | bytes 1179656 | tf_op jit(solution)/shard_map/ppermute | solution.py:508
  194.3 29.5 %collective-permute-start.26 = (f32[96,8,128]{2,1,0:T(8,128)}, f32[96,8,128]{2,1,0:T(8,128)S(1)}, u32[]{:S(2)}, u32[]{:S(2)}) collective-permute-start(f32[96,8,128]{2,1,0:T(8,128)} %get-tuple-element.120), channel_id=1, source_target_pairs={{0,96},{16,112},{32,0},{48,16},{64,32},{80,48},{96,64},{112,80},{1... | collective-permute-start | bytes 1179656 | tf_op jit(solution)/shard_map/ppermute | solution.py:508
  197.0 26.8 %collective-permute-start.27 = (f32[96,8,128]{2,1,0:T(8,128)}, f32[96,8,128]{2,1,0:T(8,128)}, u32[]{:S(2)}, u32[]{:S(2)}) collective-permute-start(f32[96,8,128]{2,1,0:T(8,128)} %get-tuple-element.121), channel_id=1, source_target_pairs={{0,112},{16,0},{32,16},{48,32},{64,48},{80,64},{96,80},{112,96},{1... | collective-permute-start | bytes 1179656 | tf_op jit(solution)/shard_map/ppermute | solution.py:508
  227.9 28.4 %collective-permute-start.29 = (f32[96,8,128]{2,1,0:T(8,128)}, f32[96,8,128]{2,1,0:T(8,128)S(1)}, u32[]{:S(2)}, u32[]{:S(2)}) collective-permute-start(f32[96,8,128]{2,1,0:T(8,128)} %collect_rows.1.rest_0_), channel_id=1, source_target_pairs={{0,32},{16,48},{32,64},{48,80},{64,96},{80,112},{96,0},{112,16},{1... | collective-permute-start | bytes 1179656 | tf_op jit(solution)/shard_map/ppermute | solution.py:508
  230.7 25.6 %collective-permute-start.30 = (f32[96,8,128]{2,1,0:T(8,128)}, f32[96,8,128]{2,1,0:T(8,128)S(1)}, u32[]{:S(2)}, u32[]{:S(2)}) collective-permute-start(f32[96,8,128]{2,1,0:T(8,128)} %collect_rows.1.rest_0_), channel_id=1, source_target_pairs={{0,48},{16,64},{32,80},{48,96},{64,112},{80,0},{96,16},{112,32},{1... | collective-permute-start | bytes 1179656 | tf_op jit(solution)/shard_map/ppermute | solution.py:508
  233.0 45.8 %collective-permute-start.31 = (f32[96,8,128]{2,1,0:T(8,128)}, f32[96,8,128]{2,1,0:T(8,128)S(1)}, u32[]{:S(2)}, u32[]{:S(2)}) collective-permute-start(f32[96,8,128]{2,1,0:T(8,128)} %collect_rows.1.rest_0_), channel_id=1, source_target_pairs={{0,64},{16,80},{32,96},{48,112},{64,0},{80,16},{96,32},{112,48},{1... | collective-permute-start | bytes 1179656 | tf_op jit(solution)/shard_map/ppermute | solution.py:508
  234.1 44.7 %collective-permute-start.32 = (f32[96,8,128]{2,1,0:T(8,128)}, f32[96,8,128]{2,1,0:T(8,128)S(1)}, u32[]{:S(2)}, u32[]{:S(2)}) collective-permute-start(f32[96,8,128]{2,1,0:T(8,128)} %collect_rows.1.rest_0_), channel_id=1, source_target_pairs={{0,80},{16,96},{32,112},{48,0},{64,16},{80,32},{96,48},{112,64},{1... | collective-permute-start | bytes 1179656 | tf_op jit(solution)/shard_map/ppermute | solution.py:508
  239.0 39.8 %collective-permute-start.33 = (f32[96,8,128]{2,1,0:T(8,128)}, f32[96,8,128]{2,1,0:T(8,128)}, u32[]{:S(2)}, u32[]{:S(2)}) collective-permute-start(f32[96,8,128]{2,1,0:T(8,128)} %collect_rows.1.rest_0_), channel_id=1, source_target_pairs={{0,96},{16,112},{32,0},{48,16},{64,32},{80,48},{96,64},{112,80},{1... | collective-permute-start | bytes 1179656 | tf_op jit(solution)/shard_map/ppermute | solution.py:508
  256.3 22.5 %collective-permute-start.34 = (f32[96,8,128]{2,1,0:T(8,128)}, f32[96,8,128]{2,1,0:T(8,128)}, u32[]{:S(2)}, u32[]{:S(2)}) collective-permute-start(f32[96,8,128]{2,1,0:T(8,128)} %collect_rows.1.rest_0_), channel_id=1, source_target_pairs={{0,112},{16,0},{32,16},{48,32},{64,48},{80,64},{96,80},{112,96},{1... | collective-permute-start | bytes 1179656 | tf_op jit(solution)/shard_map/ppermute | solution.py:508
  293.7 252.4 %all-to-all-start.1 = ((f32[256,128,128]{2,1,0:T(8,128)}), f32[256,128,128]{2,1,0:T(8,128)}, u32[]{:S(2)}, u32[]{:S(2)}) async-start(f32[256,128,128]{2,1,0:T(8,128)} %get-tuple-element.132), calls=%async_computation.1 | async-start | bytes 33554432 | tf_op jit(solution)/shard_map/all_to_all | solution.py:505
  (18 other events, 297.7 us)
Sparse Core Ops, SparseCore 0:
  174.9 118.6 all-gather.1
where the time goes:
time: 582 us; the launch traced here: 580 us
  waiting for transfers between devices  302 us (52%)
  Pallas kernels  138 us (24%)
  starting transfers between devices  71.9 us (12%)
  blocking collectives  42.9 us (7%)
  between operations  14.6 us (3%)
  other arithmetic  6.59 us (1%)
    all_to_all x1, waiting for transfers between devices, exchange(): return lax.all_to_all(x, axes, split_axis=0, concat_axis=0, tiled=True)  212 us
    ppermute x21, waiting for transfers between devices, shift(): lax.ppermute(x, 'row', [(p, (p + t) % row_count) for p in range(row_count)])  72.9 us
    ppermute x21, starting transfers between devices, shift(): lax.ppermute(x, 'row', [(p, (p + t) % row_count) for p in range(row_count)])  52.4 us
    all_to_all x1, blocking collectives, exchange(): return lax.all_to_all(x, axes, split_axis=0, concat_axis=0, tiled=True)  42.9 us
    pallas_call x1, Pallas kernels, parcel(): pl.pallas_call(parcel_body, in_specs=[SMEM, SMEM, ANY], out_specs=[vmem]...  35.7 us
    pallas_call x1, Pallas kernels, eliminate(): pl.pallas_call(main_body, grid=(parts // 2,), in_specs=[SMEM, whole3, who...  32.4 us
    pallas_call x1, Pallas kernels, add_tiles(): pl.pallas_call(tail_body, in_specs=[SMEM, ANY, ANY], out_specs=ANY, out_s...  27.4 us
    pallas_call x1, Pallas kernels, land_rows(): pl.pallas_call(body, grid=(count // 2,), in_specs=[SMEM, SMEM, SMEM, slab...  23.6 us
  transfers between devices with their start and end apart: 30, of which 12 were waited for; matrix products, arithmetic and copies ran while one was open for 1% of the time, Pallas kernels for 9%

commit v1 on v0

--- a/solution.py
+++ b/solution.py
@@ -18,7 +18,10 @@
 I32 = jnp.int32
 ANY = pl.BlockSpec(memory_space=pl.ANY)
 SMEM = pl.BlockSpec(memory_space=pltpu.SMEM)
-BIG = pltpu.CompilerParams(vmem_limit_bytes=60 * 1024 * 1024)
+
+
+def room(mib):
+    return pltpu.CompilerParams(vmem_limit_bytes=mib * 1024 * 1024)
 
 
 def halves(x):
@@ -80,13 +83,30 @@
             pltpu.SemaphoreType.DMA(()),
             pltpu.SemaphoreType.DMA(()),
         ],
-        compiler_params=BIG,
+        compiler_params=room(10),
         name="pack_tiles",
     )(owner, spot, tiles)
 
 
-def pick_body(me, place, rows, *rest):
-    outs, corner, held, sem = rest[:-3], rest[-3], rest[-2], rest[-1]
+def pick_body(me, leaving, place, rows, *rest):
+    count = (len(rest) - 4) // 2
+    parcels, outs = rest[:count], rest[count : 2 * count]
+    corner, held, sem, leave_sem = rest[2 * count :]
+    cap = parcels[0].shape[0]
+    share = outs[0].shape[0]
+    sent = jnp.int32(0)
+    for t in range(count):
+
+        def fill(i, n, t=t):
+            at = leaving[t * cap + i]
+
+            @pl.when(at >= 0)
+            def _():
+                pltpu.make_async_copy(rows.at[at], parcels[t].at[i], leave_sem).start()
+
+            return n + (at >= 0).astype(I32)
+
+        sent = lax.fori_loop(0, cap, fill, sent)
     held[...] = jnp.zeros_like(held)
 
     def go(i, n):
@@ -104,27 +124,37 @@
         pltpu.make_async_copy(rows.at[0], held.at[0], sem).wait()
         return carry
 
+    def finish_leave(i, carry):
+        pltpu.make_async_copy(rows.at[0], parcels[0].at[0], leave_sem).wait()
+        return carry
+
+    lax.fori_loop(0, sent, finish_leave, 0)
     lax.fori_loop(0, started, finish, 0)
     for g in range(2):
         corner[:, g * LANES : (g + 1) * LANES] = held[:, g, :]
     for t, out in enumerate(outs):
-        share = out.shape[0]
-        out[...] = held[pl.ds(lax.rem(me[0] + t, len(outs)) * share, share)]
-
-
-def pick(me, place, rows, count):
+        out[...] = held[pl.ds(lax.rem(me[0] + t, count) * share, share)]
+
+
+def pick(me, leaving, place, rows, count):
     total = place.shape[0]
+    cap = leaving.shape[0] // count
     vmem = pl.BlockSpec(memory_space=pltpu.VMEM)
     return pl.pallas_call(
         pick_body,
-        in_specs=[SMEM, SMEM, ANY],
-        out_specs=[vmem] * (count + 1),
-        out_shape=[jax.ShapeDtypeStruct((total // count, GROUPS, LANES), F32)] * count
+        in_specs=[SMEM, SMEM, SMEM, ANY],
+        out_specs=[vmem] * (2 * count + 1),
+        out_shape=[jax.ShapeDtypeStruct((cap, GROUPS, LANES), F32)] * count
+        + [jax.ShapeDtypeStruct((total // count, GROUPS, LANES), F32)] * count
         + [jax.ShapeDtypeStruct((total, NB), F32)],
-        scratch_shapes=[pltpu.VMEM((total, GROUPS, LANES), F32), pltpu.SemaphoreType.DMA(())],
-        compiler_params=BIG,
+        scratch_shapes=[
+            pltpu.VMEM((total, GROUPS, LANES), F32),
+            pltpu.SemaphoreType.DMA(()),
+            pltpu.SemaphoreType.DMA(()),
+        ],
+        compiler_params=room(16),
         name="pick_rows",
-    )(me, place, rows)
+    )(me, leaving, place, rows)
 
 
 def collect_body(*refs):
@@ -141,142 +171,70 @@
         in_specs=[vmem] * len(given),
         out_specs=vmem,
         out_shape=jax.ShapeDtypeStruct(given[0].shape, F32),
-        compiler_params=BIG,
+        compiler_params=room(10),
         name="collect_rows",
     )(*given)
 
 
-def parcel_body(turn, row, rows, *rest):
-    outs, seen, sem = rest[:-2], rest[-2], rest[-1]
-    for t in range(len(outs)):
-        seen[t] = 0
-
-    def go(i, n):
-        to = turn[i]
-        at = seen[jnp.maximum(to, 0)]
-        fits = (to >= 0) & (at < PARCEL)
-
-        @pl.when(fits)
-        def _():
-            seen[to] = at + 1
-            for t, out in enumerate(outs):
-
-                @pl.when(to == t)
-                def _():
-                    pltpu.make_async_copy(rows.at[row[i]], out.at[at], sem).start()
-
-        return n + fits.astype(I32)
-
-    started = lax.fori_loop(0, turn.shape[0], go, 0)
-
-    def finish(i, carry):
-        pltpu.make_async_copy(rows.at[0], outs[0].at[0], sem).wait()
-        return carry
-
-    lax.fori_loop(0, started, finish, 0)
-
-
-def parcel(turn, row, rows, count):
+def land_body(landing, rows, corner, notes, *rest):
+    parcels = rest[:-5]
+    out, parts, held, sem, out_sem = rest[-5:]
+    load = pltpu.make_async_copy(rows, held, sem)
+    load.start()
+    share = corner.shape[0] // parts.shape[0]
+    height = held.shape[0] // parts.shape[0]
+
+    def head(s, carry):
+        parts[s, height : height + share] = corner[pl.ds(pl.multiple_of(s * share, 8), share)]
+        parts[s, height + share :] = notes[s]
+        return carry
+
+    lax.fori_loop(0, parts.shape[0], head, 0)
+    load.wait()
+    for t, given in enumerate(parcels):
+        cap = given.shape[0]
+
+        def settle(i, carry, t=t, given=given, cap=cap):
+            at = landing[t * cap + i]
+
+            @pl.when(at >= 0)
+            def _():
+                held[at] = given[i]
+
+            return carry
+
+        lax.fori_loop(0, cap, settle, 0)
+    save = pltpu.make_async_copy(held, out, out_sem)
+    save.start()
+
+    def body(s, carry):
+        for g in range(2):
+            parts[s, :height, g * LANES : (g + 1) * LANES] = held[pl.ds(s * height, height), g, :]
+        return carry
+
+    lax.fori_loop(0, parts.shape[0], body, 0)
+    save.wait()
+
+
+def land_rows(landing, rows, corner, notes, parcels):
+    count = notes.shape[0]
     vmem = pl.BlockSpec(memory_space=pltpu.VMEM)
+    length = rows.shape[0] // count + corner.shape[0] // count + notes.shape[1]
     return pl.pallas_call(
-        parcel_body,
-        in_specs=[SMEM, SMEM, ANY],
-        out_specs=[vmem] * count,
-        out_shape=[jax.ShapeDtypeStruct((PARCEL, GROUPS, LANES), F32)] * count,
-        scratch_shapes=[pltpu.SMEM((count,), I32), pltpu.SemaphoreType.DMA(())],
-        compiler_params=BIG,
-        name="parcel_rows",
-    )(turn, row, rows)
-
-
-def land_body(ranked, turn, row, was, rows, corner, notes, *rest):
-    parcels = rest[:-8]
-    out, parts, stack, seen, at_row, at_turn, at_rank, total = rest[-8:]
-    step = pl.program_id(0)
-    tall = rows.shape[0]
-    height = tall // 2
-    share = corner.shape[0] // 2
-
-    @pl.when(step == 0)
-    def _():
-        for t, given in enumerate(parcels):
-            seen[t] = 0
-            stack[t] = given[...]
-
-        def note(i, n):
-            to = turn[i]
-
-            @pl.when(to >= 0)
-            def _():
-                at_row[n] = row[i]
-                at_turn[n] = to
-                rank = seen[to]
-                seen[to] = rank + 1
-                at_rank[n] = jnp.minimum(rank, PARCEL - 1) if ranked else was[i]
-
-            return n + (to >= 0).astype(I32)
-
-        total[0] = lax.fori_loop(0, turn.shape[0], note, 0)
-
-    out[...] = rows[...]
-    first = step * tall
-
-    def settle(i, carry):
-        at = at_row[i] - first
-
-        @pl.when((at >= 0) & (at < tall))
-        def _():
-            out[at] = stack[at_turn[i], at_rank[i]]
-
-        return carry
-
-    lax.fori_loop(0, total[0], settle, 0)
-    for s in range(2):
-        for g in range(2):
-            parts[s, :height, g * LANES : (g + 1) * LANES] = out[s * height : (s + 1) * height, g, :]
-        parts[s, height : height + share] = corner[s * share : (s + 1) * share]
-        parts[s, height + share :] = notes[s]
-
-
-def land_rows(turn, row, was, rows, corner, notes, parcels, ranked):
-    count = notes.shape[0]
-    tall = rows.shape[0] // count * 2
-    share = corner.shape[0] // count
-    slab = pl.BlockSpec((tall, GROUPS, LANES), lambda i: (i, 0, 0))
-    events = turn.shape[0]
-    length = tall // 2 + share + notes.shape[1]
-
-    def body(*refs):
-        return land_body(ranked, *refs)
-
-    return pl.pallas_call(
-        body,
-        grid=(count // 2,),
-        in_specs=[
-            SMEM,
-            SMEM,
-            SMEM,
-            slab,
-            pl.BlockSpec((2 * share, NB), lambda i: (i, 0)),
-            pl.BlockSpec((2,) + notes.shape[1:], lambda i: (i, 0, 0)),
-        ]
-        + [pl.BlockSpec(p.shape, lambda i: (0, 0, 0)) for p in parcels],
-        out_specs=[slab, pl.BlockSpec((2, length, NB), lambda i: (i, 0, 0))],
+        land_body,
+        in_specs=[SMEM, ANY, vmem, vmem] + [vmem] * len(parcels),
+        out_specs=[ANY, vmem],
         out_shape=[
             jax.ShapeDtypeStruct(rows.shape, F32),
             jax.ShapeDtypeStruct((count, length, NB), F32),
         ],
         scratch_shapes=[
-            pltpu.VMEM((len(parcels),) + parcels[0].shape, F32),
-            pltpu.SMEM((len(parcels),), I32),
-            pltpu.SMEM((events,), I32),
-            pltpu.SMEM((events,), I32),
-            pltpu.SMEM((events,), I32),
-            pltpu.SMEM((1,), I32),
-        ],
-        compiler_params=BIG,
-        name="land_ranked" if ranked else "land_whole",
-    )(turn, row, was, rows, corner, notes, *parcels)
+            pltpu.VMEM(rows.shape, F32),
+            pltpu.SemaphoreType.DMA(()),
+            pltpu.SemaphoreType.DMA(()),
+        ],
+        compiler_params=room(28),
+    )(landing, rows, corner, notes, *parcels)
 
 
 def main_body(me, linv, uinv, gathered, panels, block, *rest):
@@ -391,7 +349,7 @@
             pltpu.VMEM((parts, STEPS, share, NB), F32),
             pltpu.SemaphoreType.DMA(()),
         ],
-        compiler_params=BIG,
+        compiler_params=room(42),
         name="eliminate",
     )(me, linv, uinv, gathered, gathered, rows, *chunks)
 
@@ -430,18 +388,27 @@
         return carry
 
     lax.fori_loop(0, total, add, 0)
-    copies = []
-    for s in range(acc.shape[0] // GROUPS):
-        p = s % 2
-        if s >= 2:
-            copies[s - 2].wait()
+    strips = acc.shape[0] // GROUPS
+
+    def writing(s):
+        p = lax.rem(s, 2)
+        return pltpu.make_async_copy(staged.at[p], out.at[pl.ds(s * edge, edge)], out_sem.at[p])
+
+    def strip(s, carry):
+        p = lax.rem(s, 2)
+
+        @pl.when(s >= 2)
+        def _():
+            writing(s - 2).wait()
+
         for g in range(GROUPS):
             staged[p, :, g, :] = acc[s * GROUPS + g]
-        copy = pltpu.make_async_copy(staged.at[p], out.at[pl.ds(s * edge, edge)], out_sem.at[p])
-        copy.start()
-        copies.append(copy)
-    copies[-2].wait()
-    copies[-1].wait()
+        writing(s).start()
+        return carry
+
+    lax.fori_loop(0, strips, strip, 0)
+    writing(jnp.int32(strips - 2)).wait()
+    writing(jnp.int32(strips - 1)).wait()
 
 
 def add_tiles(ids, base, received):
@@ -460,7 +427,7 @@
             pltpu.SemaphoreType.DMA((RING,)),
             pltpu.SemaphoreType.DMA((2,)),
         ],
-        compiler_params=BIG,
+        compiler_params=room(14),
         name="add_tiles",
     )(ids, base, received)
 
@@ -492,6 +459,19 @@
     return source, land, jnp.concatenate([j, v1, v2])
 
 
+def ranks(turn):
+    i = jnp.arange(turn.shape[0], dtype=I32)
+    earlier = (turn[:, None] == turn[None, :]) & (i[None, :] < i[:, None])
+    return jnp.sum(earlier.astype(I32), axis=1)
+
+
+def slots(turn, rank, cap, count, value):
+    slot = jnp.where((turn >= 0) & (rank < cap), turn * cap + rank, -1)
+    place = jnp.arange(count * cap, dtype=I32)
+    same = slot[None, :] == place[:, None]
+    return jnp.sum(jnp.where(same, value[None, :] + 1, 0), axis=1) - 1
+
+
 def step(front_matrix, swap_rows, l_inverse, u_inverse, contrib_tiles, tile_owner, tile_spot):
     row_count = lax.axis_size("row")
     col_count = lax.axis_size("col")
@@ -523,21 +503,23 @@
     pair = jnp.where(land >= 0, from_row * row_count + to_row, -1)
     loads = jnp.sum((pair[:, None] == jnp.arange(STEPS * row_count, dtype=I32)[None, :]).astype(I32), axis=0)
 
-    parcels = parcel(going, old % NB, rows, row_count)
+    leaving = slots(going, ranks(going), PARCEL, row_count, old % NB)
+    landing = slots(coming, ranks(coming), PARCEL, row_count, home(land))
+    picked = pick(me, leaving, home(source), rows, row_count)
+    parcels, picked, corner = picked[:row_count], picked[row_count:-1], picked[-1]
     parcels = [parcels[0]] + [leave(parcels[t], t) for t in range(1, row_count)]
-    picked = pick(me, home(source), rows, row_count)
-    picked, corner = list(picked[:-1]), picked[-1]
     given = [picked[0]] + [shift(picked[t], t) for t in range(1, row_count)]
     send, ids = pack(contrib_tiles, tile_owner[:, 0], tile_spot, row_count * col_count)
     notes = ids.astype(F32).reshape(row_count, col_count, CAP).transpose(1, 0, 2).reshape(col_count, -1)
     notes = jnp.pad(notes[:, None, :], ((0, 0), (0, 7), (0, NB - notes.shape[1])))
 
     def ranked(parcels):
-        return land_rows(coming, home(land), old % NB, rows, corner, notes, parcels, True)
+        return land_rows(landing, rows, corner, notes, parcels)
 
     def whole(parcels):
         every = [rows[:NB]] + [leave(rows[:NB], t) for t in range(1, row_count)]
-        return land_rows(coming, home(land), old % NB, rows, corner, notes, every, False)
+        spread = slots(coming, old % NB, NB, row_count, home(land))
+        return land_rows(spread, rows, corner, notes, every)
 
     moved, parts = lax.cond(jnp.max(loads) > PARCEL, whole, ranked, parcels)
     dealt = exchange(parts, "col")

time: 582 us -> 574 us (0.986)
  Pallas kernels: 138 us -> 98.2 us
  local copies, waits for them, and re-layouts: 4.97 us -> 26.8 us
  starting transfers between devices: 71.9 us -> 79.1 us
    pallas_call x3 -> x2, Pallas kernels: 68.5 us -> 27.1 us  [the longest x1 15.1 us: land_rows(): pl.pallas_call(land_body, in_specs=[SMEM, ANY, vmem, vmem] + [vmem] * len...]
    unnamed x30 -> x68, local copies, waits for them, and re-layouts: 1.16 us -> 21.6 us
    pallas_call x1, Pallas kernels: 6.73 us -> 13.2 us  [pack(): pl.pallas_call(pack_body, in_specs=[SMEM, SMEM, ANY], out_specs=[ANY, SME...]
  transfers between devices with their start and end apart: 30 -> 30, of which waited for: 12 -> 11; matrix products, arithmetic and copies ran while one was open for 1% -> 1% of each run, Pallas kernels for 9% -> 8%
where the time goes in v1:
time: 574 us; the launch traced here: 573 us
  waiting for transfers between devices  301 us (52%)
  Pallas kernels  98.2 us (17%)
  starting transfers between devices  79.1 us (14%)
  blocking collectives  43 us (7%)
  local copies, waits for them, and re-layouts  26.8 us (5%)
  between operations  14.7 us (3%)
  other arithmetic  10.2 us (2%)
    all_to_all x1, waiting for transfers between devices, exchange(): return lax.all_to_all(x, axes, split_axis=0, concat_axis=0, tiled=True)  210 us
    ppermute x21, waiting for transfers between devices, shift(): lax.ppermute(x, 'row', [(p, (p + t) % row_count) for p in range(row_count)])  69.3 us
    ppermute x21, starting transfers between devices, shift(): lax.ppermute(x, 'row', [(p, (p + t) % row_count) for p in range(row_count)])  54.6 us
    all_to_all x1, blocking collectives, exchange(): return lax.all_to_all(x, axes, split_axis=0, concat_axis=0, tiled=True)  43 us
    pallas_call x1, Pallas kernels, eliminate(): pl.pallas_call(main_body, grid=(parts // 2,), in_specs=[SMEM, whole3, who...  31 us
    pallas_call x1, Pallas kernels, add_tiles(): pl.pallas_call(tail_body, in_specs=[SMEM, ANY, ANY], out_specs=ANY, out_s...  26.8 us
    unnamed x68, local copies, waits for them, and re-layouts  21.6 us
    ppermute x7, starting transfers between devices, leave(): lax.ppermute(x, 'row', [(p, (p + t) % row_count) for p in range(STEPS)])  16.2 us
  transfers between devices with their start and end apart: 30, of which 11 were waited for; matrix products, arithmetic and copies ran while one was open for 1% of the time, Pallas kernels for 8%

profile of v1, /device:TPU:12, one launch (start us, length us, event | category | flops | bytes accessed | tf_op | source)
XLA Modules:
  0.0 572.8 jit_solution(4263140872698156780)
XLA Ops:
  10.6 12.0 %pick_rows.1 = (f32[48,8,128]{2,1,0:T(8,128)S(1)}, f32[48,8,128]{2,1,0:T(8,128)S(1)}, f32[48,8,128]{2,1,0:T(8,128)S(1)}, f32[48,8,128]{2,1,0:T(8,128)S(1)}, f32[...) custom-call(s32[2]{0:T(128)S(1)} %pad_add_fusion.8.me, ...), custom_call_target="tpu_custom_call" | custom-call | tf_op jit(solution)/shard_map/pick_rows/pallas_call | solution.py:143
  28.7 3.7 collective-permute-start.10
  41.7 13.2 %pack_tiles.1 = (f32[256,128,128]{2,1,0:T(8,128)S(1)}, s32[256]{0:T(256)S(1)}) custom-call(s32[96]{0:T(128)S(1)} %bitcast.40, s32[96]{0:T(128)S(1)} %copy-done.14, f32[96,128,128]{2,1,0:T(8,128)S(1)} %copy-done.2), custom_call_target="tpu_custom_call" | custom-call | tf_op jit(solution)/shard_map/pack_tiles/pallas_call | solution.py:72
  55.0 5.7 %copy-done.1 = f32[256,128,128]{2,1,0:T(8,128)} copy-done((f32[256,128,128]{2,1,0:T(8,128)}, f32[256,128,128]{2,1,0:T(8,128)S(1)}, u32[]{:S(2)}) %copy-start.1) | copy-done | bytes 16777240
  67.6 6.2 %collective-permute-done.8 = f32[48,8,128]{2,1,0:T(8,128)S(1)} collective-permute-done((f32[48,8,128]{2,1,0:T(8,128)S(1)}, f32[48,8,128]{2,1,0:T(8,128)S(1)}, u32[]{:S(2)}, u32[]{:S(2)}) %collective-permute-start.8) | collective-permute-done | bytes 196640 | tf_op jit(solution)/shard_map/ppermute | solution.py:491
  75.7 19.6 %conditional.1 = ((f32[2048,8,128]{2,1,0:T(8,128)}, f32[16,184,256]{2,1,0:T(8,128)})) conditional(s32[]{:T(128)} %convert_element_type.25, (s32[1,768]{1,0:T(1,128)S(1)}, s32[1,768]{1,0:T(1,128)S(1)}, pred[1,768]{1,0:T(4,128)(4,1)S(1)}, pred[1,768]{1,0:T(4,128)(4,1)S(1)}, s32[1,768]{1,0:T(1,128)S(1)}, /*index=5*/s32[1,768]{1,0:T(1,128)S(1)}, ...), branch_computations={%region_10.13_spmd, %region_13.15_spmd} | conditional | flops 4776960 | bytes 35451228 | solution.py:524
  80.2 15.1 %branch_0_fun.1 = (f32[2048,8,128]{2,1,0:T(8,128)}, f32[16,184,256]{2,1,0:T(8,128)}) custom-call(s32[384]{0:T(512)S(1)} %sub.79.landing, f32[2048,8,128]{2,1,0:T(8,128)} %get-tuple-element.232.rows, f32[768,256]{1,0:T(8,128)S(1)} %get-tuple-element.233.corner, f32[16,8,256]{2,1,0:T(8,128)S(1)} %copy.37.notes, f32[48,8,128]{2,1,0:T(8,128)S(1)} %get-tuple-element.235.rest_0_, ...), custom_call_target="tpu_custom_call" | custom-call | tf_op jit(solution)/shard_map/cond/branch_0_fun/pallas_call | solution.py:223
  95.3 43.0 %all_to_all.10 = f32[16,184,256]{2,1,0:T(8,128)S(1)} all-to-all(f32[16,184,256]{2,1,0:T(8,128)} %get-tuple-element.296), channel_id=1, replica_groups=mesh['row'=8,'col'=16] {'col'}, dimensions={0} | all-to-all | bytes 6029312 | tf_op jit(solution)/shard_map/all_to_all | solution.py:485
  138.6 3.5 collective-permute-start.14
  146.3 3.5 collective-permute-start.17
  150.2 6.5 %collective-permute-start.19 = (f32[152,256]{1,0:T(8,128)S(1)}, f32[152,256]{1,0:T(8,128)S(1)}, u32[]{:S(2)}, u32[]{:S(2)}) collective-permute-start(f32[152,256]{1,0:T(8,128)S(1)} %select_maximum_fusion), channel_id=1, source_target_pairs={{0,96},{16,112},{32,0},{48,16},{64,32},{80,48},{96,64},{112,80},{1... | collective-permute-start | bytes 466952 | tf_op jit(solution)/shard_map/ppermute | solution.py:488
  156.8 4.5 collective-permute-done.17
  169.9 3.5 collective-permute-start.24
  173.5 10.5 %collective-permute-done.21.refs_1_ = f32[96,8,128]{2,1,0:T(8,128)S(1)} collective-permute-done((f32[96,8,128]{2,1,0:T(8,128)S(1)}, f32[96,8,128]{2,1,0:T(8,128)S(1)}, u32[]{:S(2)}, u32[]{:S(2)}) %collective-permute-start.21) | collective-permute-done | bytes 393248 | tf_op jit(solution)/shard_map/ppermute | solution.py:488
  186.3 12.1 %collective-permute-done.23.refs_3_ = f32[96,8,128]{2,1,0:T(8,128)S(1)} collective-permute-done((f32[96,8,128]{2,1,0:T(8,128)S(1)}, f32[96,8,128]{2,1,0:T(8,128)S(1)}, u32[]{:S(2)}, u32[]{:S(2)}) %collective-permute-start.23) | collective-permute-done | bytes 393248 | tf_op jit(solution)/shard_map/ppermute | solution.py:488
  198.4 14.5 %collective-permute-done.24.refs_4_ = f32[96,8,128]{2,1,0:T(8,128)S(1)} collective-permute-done((f32[96,8,128]{2,1,0:T(8,128)S(1)}, f32[96,8,128]{2,1,0:T(8,128)S(1)}, u32[]{:S(2)}, u32[]{:S(2)}) %collective-permute-start.24) | collective-permute-done | bytes 393248 | tf_op jit(solution)/shard_map/ppermute | solution.py:488
  213.5 3.5 collective-permute-start.29
  224.2 17.3 %collective-permute-start.33 = (f32[96,8,128]{2,1,0:T(8,128)S(1)}, f32[96,8,128]{2,1,0:T(8,128)S(1)}, u32[]{:S(2)}, u32[]{:S(2)}) collective-permute-start(f32[96,8,128]{2,1,0:T(8,128)S(1)} %collect_rows.1.rest_0_), channel_id=1, source_target_pairs={{0,96},{16,112},{32,0},{48,16},{64,32},{80,48},{96,64},{112,80},{1... | collective-permute-start | bytes 1179656 | tf_op jit(solution)/shard_map/ppermute | solution.py:488
  241.5 22.7 %collective-permute-done.31.rest_4_ = f32[96,8,128]{2,1,0:T(8,128)S(1)} collective-permute-done((f32[96,8,128]{2,1,0:T(8,128)S(1)}, f32[96,8,128]{2,1,0:T(8,128)S(1)}, u32[]{:S(2)}, u32[]{:S(2)}) %collective-permute-start.31) | collective-permute-done | bytes 393248 | tf_op jit(solution)/shard_map/ppermute | solution.py:488
  266.6 15.0 %all-gather.2.cloned.1.call-done = f32[8448,256]{1,0:T(8,128)} async-done(((f32[528,256]{1,0:T(8,128)}), f32[8448,256]{1,0:T(8,128)}) %all-gather.2.cloned.1.call-update) | async-done | bytes 8650768 | tf_op jit(solution)/shard_map/all_gather | solution.py:534
  281.6 8.4 %all-to-all-start.1 = ((f32[256,128,128]{2,1,0:T(8,128)}), f32[256,128,128]{2,1,0:T(8,128)}, u32[]{:S(2)}, u32[]{:S(2)}) async-start(f32[256,128,128]{2,1,0:T(8,128)} %copy-done.1), calls=%async_computation.1 | async-start | bytes 33554432 | tf_op jit(solution)/shard_map/all_to_all | solution.py:485
  294.6 31.0 %eliminate.1 = f32[16,8,128,128]{3,2,1,0:T(8,128)} custom-call(s32[2]{0:T(128)S(1)} %pad_add_fusion.8.me, f32[3,256,256]{2,1,0:T(8,128)S(1)} %copy-done.3, f32[3,256,256]{2,1,0:T(8,128)S(1)} %copy-done.4, f32[16,3,176,256]{3,2,1,0:T(8,128)} %bitcast.44, f32[16,3,176,256]{3,2,1,0:T(8,128)} %bitcast.45, f32[2048,8,128]{2,1,0:T(8,128)} %get-tuple-element.307.block, ...), custom_call_target="tpu_custom_call" | custom-call | tf_op jit(solution)/shard_map/eliminate/pallas_call | solution.py:328
  325.6 210.2 %all-to-all-done.1.received = f32[256,128,128]{2,1,0:T(8,128)} async-done(((f32[256,128,128]{2,1,0:T(8,128)}), f32[256,128,128]{2,1,0:T(8,128)}, u32[]{:S(2)}, u32[]{:S(2)}) %all-to-all-start.1) | async-done | bytes 16777248 | tf_op jit(solution)/shard_map/all_to_all | solution.py:485
  539.1 26.8 %add_tiles.1 = f32[2048,8,128]{2,1,0:T(8,128)} custom-call(s32[256]{0:T(256)S(1)} %convert_element_type.30.ids, f32[128,128,128]{2,1,0:T(8,128)S(1)} %bitcast.39, f32[256,128,128]{2,1,0:T(8,128)} %all-to-all-done.1.received), custom_call_target="tpu_custom_call" | custom-call | tf_op jit(solution)/shard_map/add_tiles/pallas_call | solution.py:416
  (192 shorter events, 65.6 us)
Async XLA Ops:
  6.5 275.0 %all-gather.2.cloned.1.call-start = ((), (), s32[]{:S(2)}) async-start(), calls=%async_computation.2 | async-start | bytes 9191424 | tf_op jit(solution)/shard_map/all_gather | solution.py:534
  28.7 35.6 %collective-permute-start.10 = (f32[48,8,128]{2,1,0:T(8,128)S(1)}, f32[48,8,128]{2,1,0:T(8,128)}, u32[]{:S(2)}, u32[]{:S(2)}) collective-permute-start(f32[48,8,128]{2,1,0:T(8,128)S(1)} %get-tuple-element.292), channel_id=1, source_target_pairs={{0,64},{16,80},{32,96},{1,65},{17,81},{33,97},{2,66},{18,82},{34,9... | collective-permute-start | bytes 589832 | tf_op jit(solution)/shard_map/ppermute | solution.py:491
  32.4 33.8 %collective-permute-start.11 = (f32[48,8,128]{2,1,0:T(8,128)S(1)}, f32[48,8,128]{2,1,0:T(8,128)}, u32[]{:S(2)}, u32[]{:S(2)}) collective-permute-start(f32[48,8,128]{2,1,0:T(8,128)S(1)} %get-tuple-element.293), channel_id=1, source_target_pairs={{0,80},{16,96},{32,112},{1,81},{17,97},{33,113},{2,82},{18,98},{34... | collective-permute-start | bytes 589832 | tf_op jit(solution)/shard_map/ppermute | solution.py:491
  34.4 33.2 %collective-permute-start.12 = (f32[48,8,128]{2,1,0:T(8,128)S(1)}, f32[48,8,128]{2,1,0:T(8,128)}, u32[]{:S(2)}, u32[]{:S(2)}) collective-permute-start(f32[48,8,128]{2,1,0:T(8,128)S(1)} %get-tuple-element.294), channel_id=1, source_target_pairs={{0,96},{16,112},{32,0},{1,97},{17,113},{33,1},{2,98},{18,114},{34,... | collective-permute-start | bytes 589832 | tf_op jit(solution)/shard_map/ppermute | solution.py:491
  37.8 29.8 %collective-permute-start.13 = (f32[48,8,128]{2,1,0:T(8,128)S(1)}, f32[48,8,128]{2,1,0:T(8,128)}, u32[]{:S(2)}, u32[]{:S(2)}) collective-permute-start(f32[48,8,128]{2,1,0:T(8,128)S(1)} %get-tuple-element.295), channel_id=1, source_target_pairs={{0,112},{16,0},{32,16},{1,113},{17,1},{33,17},{2,114},{18,2},{34,1... | collective-permute-start | bytes 589832 | tf_op jit(solution)/shard_map/ppermute | solution.py:491
  39.8 27.9 %collective-permute-start.7 = (f32[48,8,128]{2,1,0:T(8,128)S(1)}, f32[48,8,128]{2,1,0:T(8,128)}, u32[]{:S(2)}, u32[]{:S(2)}) collective-permute-start(f32[48,8,128]{2,1,0:T(8,128)S(1)} %get-tuple-element.289), channel_id=1, source_target_pairs={{0,16},{16,32},{32,48},{1,17},{17,33},{33,49},{2,18},{18,34},{34,5... | collective-permute-start | bytes 589832 | tf_op jit(solution)/shard_map/ppermute | solution.py:491
  142.2 14.5 %collective-permute-start.15 = (f32[152,256]{1,0:T(8,128)S(1)}, f32[152,256]{1,0:T(8,128)S(1)}, u32[]{:S(2)}, u32[]{:S(2)}) collective-permute-start(f32[152,256]{1,0:T(8,128)S(1)} %select_maximum_fusion), channel_id=1, source_target_pairs={{0,32},{16,48},{32,64},{48,80},{64,96},{80,112},{96,0},{112,16},{1... | collective-permute-start | bytes 466952 | tf_op jit(solution)/shard_map/ppermute | solution.py:488
  144.3 12.5 %collective-permute-start.16 = (f32[152,256]{1,0:T(8,128)S(1)}, f32[152,256]{1,0:T(8,128)S(1)}, u32[]{:S(2)}, u32[]{:S(2)}) collective-permute-start(f32[152,256]{1,0:T(8,128)S(1)} %select_maximum_fusion), channel_id=1, source_target_pairs={{0,48},{16,64},{32,80},{48,96},{64,112},{80,0},{96,16},{112,32},{1... | collective-permute-start | bytes 466952 | tf_op jit(solution)/shard_map/ppermute | solution.py:488
  146.3 15.0 %collective-permute-start.17 = (f32[152,256]{1,0:T(8,128)S(1)}, f32[152,256]{1,0:T(8,128)S(1)}, u32[]{:S(2)}, u32[]{:S(2)}) collective-permute-start(f32[152,256]{1,0:T(8,128)S(1)} %select_maximum_fusion), channel_id=1, source_target_pairs={{0,64},{16,80},{32,96},{48,112},{64,0},{80,16},{96,32},{112,48},{1... | collective-permute-start | bytes 466952 | tf_op jit(solution)/shard_map/ppermute | solution.py:488
  150.2 12.7 %collective-permute-start.19 = (f32[152,256]{1,0:T(8,128)S(1)}, f32[152,256]{1,0:T(8,128)S(1)}, u32[]{:S(2)}, u32[]{:S(2)}) collective-permute-start(f32[152,256]{1,0:T(8,128)S(1)} %select_maximum_fusion), channel_id=1, source_target_pairs={{0,96},{16,112},{32,0},{48,16},{64,32},{80,48},{96,64},{112,80},{1... | collective-permute-start | bytes 466952 | tf_op jit(solution)/shard_map/ppermute | solution.py:488
  164.2 19.8 %collective-permute-start.21 = (f32[96,8,128]{2,1,0:T(8,128)S(1)}, f32[96,8,128]{2,1,0:T(8,128)S(1)}, u32[]{:S(2)}, u32[]{:S(2)}) collective-permute-start(f32[96,8,128]{2,1,0:T(8,128)S(1)} %copy-done.28), channel_id=1, source_target_pairs={{0,16},{16,32},{32,48},{48,64},{64,80},{80,96},{96,112},{112,0},{1... | collective-permute-start | bytes 1179656 | tf_op jit(solution)/shard_map/ppermute | solution.py:488
  166.5 19.8 %collective-permute-start.22 = (f32[96,8,128]{2,1,0:T(8,128)S(1)}, f32[96,8,128]{2,1,0:T(8,128)S(1)}, u32[]{:S(2)}, u32[]{:S(2)}) collective-permute-start(f32[96,8,128]{2,1,0:T(8,128)S(1)} %copy-done.26), channel_id=1, source_target_pairs={{0,32},{16,48},{32,64},{48,80},{64,96},{80,112},{96,0},{112,16},{1... | collective-permute-start | bytes 1179656 | tf_op jit(solution)/shard_map/ppermute | solution.py:488
  168.0 30.4 %collective-permute-start.23 = (f32[96,8,128]{2,1,0:T(8,128)S(1)}, f32[96,8,128]{2,1,0:T(8,128)S(1)}, u32[]{:S(2)}, u32[]{:S(2)}) collective-permute-start(f32[96,8,128]{2,1,0:T(8,128)S(1)} %copy-done.24), channel_id=1, source_target_pairs={{0,48},{16,64},{32,80},{48,96},{64,112},{80,0},{96,16},{112,32},{1... | collective-permute-start | bytes 1179656 | tf_op jit(solution)/shard_map/ppermute | solution.py:488
  169.9 43.0 %collective-permute-start.24 = (f32[96,8,128]{2,1,0:T(8,128)S(1)}, f32[96,8,128]{2,1,0:T(8,128)S(1)}, u32[]{:S(2)}, u32[]{:S(2)}) collective-permute-start(f32[96,8,128]{2,1,0:T(8,128)S(1)} %copy-done.22), channel_id=1, source_target_pairs={{0,64},{16,80},{32,96},{48,112},{64,0},{80,16},{96,32},{112,48},{1... | collective-permute-start | bytes 1179656 | tf_op jit(solution)/shard_map/ppermute | solution.py:488
  173.4 39.5 %collective-permute-start.25 = (f32[96,8,128]{2,1,0:T(8,128)S(1)}, f32[96,8,128]{2,1,0:T(8,128)S(1)}, u32[]{:S(2)}, u32[]{:S(2)}) collective-permute-start(f32[96,8,128]{2,1,0:T(8,128)S(1)} %copy-done.20), channel_id=1, source_target_pairs={{0,80},{16,96},{32,112},{48,0},{64,16},{80,32},{96,48},{112,64},{1... | collective-permute-start | bytes 1179656 | tf_op jit(solution)/shard_map/ppermute | solution.py:488
  184.0 28.9 %collective-permute-start.26 = (f32[96,8,128]{2,1,0:T(8,128)S(1)}, f32[96,8,128]{2,1,0:T(8,128)S(1)}, u32[]{:S(2)}, u32[]{:S(2)}) collective-permute-start(f32[96,8,128]{2,1,0:T(8,128)S(1)} %copy-done.18), channel_id=1, source_target_pairs={{0,96},{16,112},{32,0},{48,16},{64,32},{80,48},{96,64},{112,80},{1... | collective-permute-start | bytes 1179656 | tf_op jit(solution)/shard_map/ppermute | solution.py:488
  186.3 26.6 %collective-permute-start.27 = (f32[96,8,128]{2,1,0:T(8,128)S(1)}, f32[96,8,128]{2,1,0:T(8,128)S(1)}, u32[]{:S(2)}, u32[]{:S(2)}) collective-permute-start(f32[96,8,128]{2,1,0:T(8,128)S(1)} %copy-done.16), channel_id=1, source_target_pairs={{0,112},{16,0},{32,16},{48,32},{64,48},{80,64},{96,80},{112,96},{1... | collective-permute-start | bytes 1179656 | tf_op jit(solution)/shard_map/ppermute | solution.py:488
  213.5 28.1 %collective-permute-start.29 = (f32[96,8,128]{2,1,0:T(8,128)S(1)}, f32[96,8,128]{2,1,0:T(8,128)S(1)}, u32[]{:S(2)}, u32[]{:S(2)}) collective-permute-start(f32[96,8,128]{2,1,0:T(8,128)S(1)} %collect_rows.1.rest_0_), channel_id=1, source_target_pairs={{0,32},{16,48},{32,64},{48,80},{64,96},{80,112},{96,0},{112,16},{1... | collective-permute-start | bytes 1179656 | tf_op jit(solution)/shard_map/ppermute | solution.py:488
  217.0 24.6 %collective-permute-start.30 = (f32[96,8,128]{2,1,0:T(8,128)S(1)}, f32[96,8,128]{2,1,0:T(8,128)S(1)}, u32[]{:S(2)}, u32[]{:S(2)}) collective-permute-start(f32[96,8,128]{2,1,0:T(8,128)S(1)} %collect_rows.1.rest_0_), channel_id=1, source_target_pairs={{0,48},{16,64},{32,80},{48,96},{64,112},{80,0},{96,16},{112,32},{1... | collective-permute-start | bytes 1179656 | tf_op jit(solution)/shard_map/ppermute | solution.py:488
  217.9 46.3 %collective-permute-start.31 = (f32[96,8,128]{2,1,0:T(8,128)S(1)}, f32[96,8,128]{2,1,0:T(8,128)S(1)}, u32[]{:S(2)}, u32[]{:S(2)}) collective-permute-start(f32[96,8,128]{2,1,0:T(8,128)S(1)} %collect_rows.1.rest_0_), channel_id=1, source_target_pairs={{0,64},{16,80},{32,96},{48,112},{64,0},{80,16},{96,32},{112,48},{1... | collective-permute-start | bytes 1179656 | tf_op jit(solution)/shard_map/ppermute | solution.py:488
  219.6 44.7 %collective-permute-start.32 = (f32[96,8,128]{2,1,0:T(8,128)S(1)}, f32[96,8,128]{2,1,0:T(8,128)S(1)}, u32[]{:S(2)}, u32[]{:S(2)}) collective-permute-start(f32[96,8,128]{2,1,0:T(8,128)S(1)} %collect_rows.1.rest_0_), channel_id=1, source_target_pairs={{0,80},{16,96},{32,112},{48,0},{64,16},{80,32},{96,48},{112,64},{1... | collective-permute-start | bytes 1179656 | tf_op jit(solution)/shard_map/ppermute | solution.py:488
  224.2 40.8 %collective-permute-start.33 = (f32[96,8,128]{2,1,0:T(8,128)S(1)}, f32[96,8,128]{2,1,0:T(8,128)S(1)}, u32[]{:S(2)}, u32[]{:S(2)}) collective-permute-start(f32[96,8,128]{2,1,0:T(8,128)S(1)} %collect_rows.1.rest_0_), channel_id=1, source_target_pairs={{0,96},{16,112},{32,0},{48,16},{64,32},{80,48},{96,64},{112,80},{1... | collective-permute-start | bytes 1179656 | tf_op jit(solution)/shard_map/ppermute | solution.py:488
  241.5 24.3 %collective-permute-start.34 = (f32[96,8,128]{2,1,0:T(8,128)S(1)}, f32[96,8,128]{2,1,0:T(8,128)S(1)}, u32[]{:S(2)}, u32[]{:S(2)}) collective-permute-start(f32[96,8,128]{2,1,0:T(8,128)S(1)} %collect_rows.1.rest_0_), channel_id=1, source_target_pairs={{0,112},{16,0},{32,16},{48,32},{64,48},{80,64},{96,80},{112,96},{1... | collective-permute-start | bytes 1179656 | tf_op jit(solution)/shard_map/ppermute | solution.py:488
  281.6 254.2 %all-to-all-start.1 = ((f32[256,128,128]{2,1,0:T(8,128)}), f32[256,128,128]{2,1,0:T(8,128)}, u32[]{:S(2)}, u32[]{:S(2)}) async-start(f32[256,128,128]{2,1,0:T(8,128)} %copy-done.1), calls=%async_computation.1 | async-start | bytes 33554432 | tf_op jit(solution)/shard_map/all_to_all | solution.py:485
  (38 other events, 315.8 us)
Sparse Core Ops, SparseCore 0:
  164.3 117.2 all-gather.1

commit v2 on v1

--- a/solution.py
+++ b/solution.py
@@ -36,56 +36,35 @@
     return one(a[0], b[0]) + (one(a[0], b[1]) + one(a[1], b[0]))
 
 
-def pack_body(owner, spot, tiles, *rest):
-    send, ids, held, seen, load_sem, sem = rest[-6:]
+def pack_body(slot, tiles, send, held, load_sem, sem):
     count = tiles.shape[0]
     load = pltpu.make_async_copy(tiles, held, load_sem)
     load.start()
-
-    def clear(i, carry):
-        ids[i] = -1
-        return carry
-
-    def fresh(i, carry):
-        seen[i] = 0
-        return carry
-
-    lax.fori_loop(0, ids.shape[0], clear, 0)
-    lax.fori_loop(0, seen.shape[0], fresh, 0)
     load.wait()
 
     def put(i, carry):
-        d = owner[i]
-        rank = seen[d]
-        seen[d] = rank + 1
-        slot = d * CAP + rank
-        ids[slot] = spot[i]
-        pltpu.make_async_copy(held.at[i], send.at[slot], sem).start()
+        pltpu.make_async_copy(held.at[i], send.at[slot[i]], sem).start()
         return carry
 
     lax.fori_loop(0, count, put, 0)
     pltpu.make_async_copy(held, send.at[pl.ds(0, count)], sem).wait()
 
 
-def pack(tiles, owner, spot, devices):
+def pack(tiles, slot, total):
     edge = tiles.shape[1]
     return pl.pallas_call(
         pack_body,
-        in_specs=[SMEM, SMEM, ANY],
-        out_specs=[ANY, SMEM],
-        out_shape=[
-            jax.ShapeDtypeStruct((devices * CAP, edge, edge), F32),
-            jax.ShapeDtypeStruct((devices * CAP,), I32),
-        ],
+        in_specs=[SMEM, ANY],
+        out_specs=ANY,
+        out_shape=jax.ShapeDtypeStruct((total, edge, edge), F32),
         scratch_shapes=[
             pltpu.VMEM(tiles.shape, F32),
-            pltpu.SMEM((devices,), I32),
             pltpu.SemaphoreType.DMA(()),
             pltpu.SemaphoreType.DMA(()),
         ],
         compiler_params=room(10),
         name="pack_tiles",
-    )(owner, spot, tiles)
+    )(slot, tiles)
 
 
 def pick_body(me, leaving, place, rows, *rest):
@@ -237,9 +216,9 @@
     )(landing, rows, corner, notes, *parcels)
 
 
-def main_body(me, linv, uinv, gathered, panels, block, *rest):
-    chunks = rest[:-9]
-    out, chosen, final, upper, upper_hi, upper_lo, factor, corner, sem = rest[-9:]
+def main_body(me, linv, uinv, gathered, panels, block, tiles, *rest):
+    chunks = rest[:-10]
+    done, out, chosen, final, upper, upper_hi, upper_lo, factor, corner, sem = rest[-10:]
     step = pl.program_id(0)
     height = panels.shape[2]
 
@@ -318,8 +297,12 @@
             for g in range(2):
                 out[s, g] = final[me[0], me[1], s * height : (s + 1) * height, g * LANES : (g + 1) * LANES]
 
-
-def eliminate(me, linv, uinv, gathered, rows, chunks):
+    for s in range(2):
+        for g in range(GROUPS):
+            done[s * height : (s + 1) * height, g, :] = out[s, g] + tiles[s * GROUPS + g]
+
+
+def eliminate(me, linv, uinv, gathered, rows, tiles, chunks):
     parts, _, both, _ = gathered.shape
     height = rows.shape[0] // parts
     share = both - height
@@ -335,11 +318,13 @@
             ANY,
             pl.BlockSpec((2, STEPS, height, NB), lambda i: (i, 0, 0, 0)),
             pl.BlockSpec((2 * height, GROUPS, LANES), lambda i: (i, 0, 0)),
+            pl.BlockSpec((2 * GROUPS, height, LANES), lambda i: (i, 0, 0)),
         ]
         + [pl.BlockSpec(c.shape, lambda i: (0, 0, 0)) for c in chunks],
-        out_specs=pl.BlockSpec((2, GROUPS, height, LANES), lambda i: (i, 0, 0, 0)),
-        out_shape=jax.ShapeDtypeStruct((parts, GROUPS, height, LANES), F32),
+        out_specs=pl.BlockSpec((2 * height, GROUPS, LANES), lambda i: (i, 0, 0)),
+        out_shape=jax.ShapeDtypeStruct(rows.shape, F32),
         scratch_shapes=[
+            pltpu.VMEM((2, GROUPS, height, LANES), F32),
             pltpu.VMEM((STEPS * NB, GROUPS, LANES), F32),
             pltpu.VMEM((STEPS, STEPS, NB, NB), F32),
             pltpu.VMEM((STEPS * NB, width), F32),
@@ -351,14 +336,10 @@
         ],
         compiler_params=room(42),
         name="eliminate",
-    )(me, linv, uinv, gathered, gathered, rows, *chunks)
-
-
-def tail_body(ids, base, received, out, acc, ring, staged, order, base_sem, ring_sem, out_sem):
-    whole = pltpu.make_async_copy(base, acc, base_sem)
-    whole.start()
-    edge = acc.shape[1]
-
+    )(me, linv, uinv, gathered, gathered, rows, tiles, *chunks)
+
+
+def sum_body(ids, received, out, acc, ring, order, ring_sem, out_sem):
     def note(i, n):
         order[n] = i
         return n + (ids[i] >= 0).astype(I32)
@@ -374,7 +355,12 @@
         return carry
 
     lax.fori_loop(0, jnp.minimum(total, RING), prime, 0)
-    whole.wait()
+
+    def clear(m, carry):
+        acc[m] = jnp.zeros(acc.shape[1:], F32)
+        return carry
+
+    lax.fori_loop(0, acc.shape[0], clear, 0)
 
     def add(j, carry):
         fetch(j).wait()
@@ -388,48 +374,28 @@
         return carry
 
     lax.fori_loop(0, total, add, 0)
-    strips = acc.shape[0] // GROUPS
-
-    def writing(s):
-        p = lax.rem(s, 2)
-        return pltpu.make_async_copy(staged.at[p], out.at[pl.ds(s * edge, edge)], out_sem.at[p])
-
-    def strip(s, carry):
-        p = lax.rem(s, 2)
-
-        @pl.when(s >= 2)
-        def _():
-            writing(s - 2).wait()
-
-        for g in range(GROUPS):
-            staged[p, :, g, :] = acc[s * GROUPS + g]
-        writing(s).start()
-        return carry
-
-    lax.fori_loop(0, strips, strip, 0)
-    writing(jnp.int32(strips - 2)).wait()
-    writing(jnp.int32(strips - 1)).wait()
-
-
-def add_tiles(ids, base, received):
-    spots, edge, _ = base.shape
+    copy = pltpu.make_async_copy(acc, out, out_sem)
+    copy.start()
+    copy.wait()
+
+
+def sum_tiles(ids, received, spots):
+    edge = received.shape[1]
     return pl.pallas_call(
-        tail_body,
-        in_specs=[SMEM, ANY, ANY],
+        sum_body,
+        in_specs=[SMEM, ANY],
         out_specs=ANY,
-        out_shape=jax.ShapeDtypeStruct((spots // GROUPS * edge, GROUPS, LANES), F32),
+        out_shape=jax.ShapeDtypeStruct((spots, edge, LANES), F32),
         scratch_shapes=[
             pltpu.VMEM((spots, edge, LANES), F32),
             pltpu.VMEM((RING, edge, LANES), F32),
-            pltpu.VMEM((2, edge, GROUPS, LANES), F32),
             pltpu.SMEM((ids.shape[0],), I32),
-            pltpu.SemaphoreType.DMA(()),
             pltpu.SemaphoreType.DMA((RING,)),
-            pltpu.SemaphoreType.DMA((2,)),
+            pltpu.SemaphoreType.DMA(()),
         ],
         compiler_params=room(14),
-        name="add_tiles",
-    )(ids, base, received)
+        name="sum_tiles",
+    )(ids, received)
 
 
 def look(x, t, values, other):
@@ -503,13 +469,17 @@
     pair = jnp.where(land >= 0, from_row * row_count + to_row, -1)
     loads = jnp.sum((pair[:, None] == jnp.arange(STEPS * row_count, dtype=I32)[None, :]).astype(I32), axis=0)
 
+    owners = tile_owner[:, 0]
+    slot = owners * CAP + jnp.minimum(ranks(owners), CAP - 1)
+    total = row_count * col_count * CAP
+    ids = slots(owners, slot - owners * CAP, CAP, row_count * col_count, tile_spot)
     leaving = slots(going, ranks(going), PARCEL, row_count, old % NB)
     landing = slots(coming, ranks(coming), PARCEL, row_count, home(land))
     picked = pick(me, leaving, home(source), rows, row_count)
     parcels, picked, corner = picked[:row_count], picked[row_count:-1], picked[-1]
     parcels = [parcels[0]] + [leave(parcels[t], t) for t in range(1, row_count)]
     given = [picked[0]] + [shift(picked[t], t) for t in range(1, row_count)]
-    send, ids = pack(contrib_tiles, tile_owner[:, 0], tile_spot, row_count * col_count)
+    send = pack(contrib_tiles, slot, total)
     notes = ids.astype(F32).reshape(row_count, col_count, CAP).transpose(1, 0, 2).reshape(col_count, -1)
     notes = jnp.pad(notes[:, None, :], ((0, 0), (0, 7), (0, NB - notes.shape[1])))
 
@@ -521,6 +491,7 @@
         spread = slots(coming, old % NB, NB, row_count, home(land))
         return land_rows(spread, rows, corner, notes, every)
 
+    parcels, landing = lax.optimization_barrier((parcels, landing))
     moved, parts = lax.cond(jnp.max(loads) > PARCEL, whole, ranked, parcels)
     dealt = exchange(parts, "col")
     tall = local_rows // col_count
@@ -531,18 +502,19 @@
     partial = jnp.stack([partial] + [shift(partial, t) for t in range(1, row_count)])
     corner = jnp.sum(partial[:, :-8], axis=0).reshape(STEPS, -1, NB)
     mixed = jnp.concatenate([dealt[:STEPS, :tall], corner], axis=1)
-    gathered = lax.all_gather(mixed.reshape(-1, NB), "col", axis=0, tiled=True)
-    gathered = gathered.reshape(col_count, STEPS, -1, NB)
     notes = partial[:, -8].reshape(row_count, -1)[:, : row_count * col_count * CAP]
     notes = lax.dynamic_slice_in_dim(notes, row_place * col_count * CAP, col_count * CAP, 1)
     turn = (row_place - jnp.arange(row_count, dtype=I32)) % row_count
     ids_in = notes[turn].reshape(-1).astype(I32)
+    send, mixed, ids_in, *given = lax.optimization_barrier((send, mixed, ids_in, *given))
+    received = exchange(send, ("row", "col"))
+    received, mixed, *given = lax.optimization_barrier((received, mixed, *given))
+    gathered = lax.all_gather(mixed.reshape(-1, NB), "col", axis=0, tiled=True)
+    gathered = gathered.reshape(col_count, STEPS, -1, NB)
     summed = collect(given)
     chunks = [summed] + [shift(summed, t) for t in range(1, row_count)]
-    send, gathered, *chunks = lax.optimization_barrier((send, gathered, *chunks))
-    received = exchange(send, ("row", "col"))
-    base = eliminate(me, l_inverse, u_inverse, gathered, moved, chunks)
-    out = add_tiles(ids_in, base.reshape(-1, LANES, LANES), received)
+    tiles = sum_tiles(ids_in, received, local_rows // LANES * GROUPS)
+    out = eliminate(me, l_inverse, u_inverse, gathered, moved, tiles, chunks)
     return out.reshape(-1).reshape(front_matrix.shape)
 
 

time: 574 us -> 585 us (1.019)
  the two profiles are of different devices: /device:TPU:12 before, /device:TPU:30 now
where the time goes in v2:
time: 585 us; the launch traced here: 577 us
  blocking collectives  212 us (36%)
  waiting for transfers between devices  163 us (28%)
  Pallas kernels  82 us (14%)
  starting transfers between devices  58.3 us (10%)
  local copies, waits for them, and re-layouts  40.5 us (7%)
  between operations  14.7 us (3%)
  other arithmetic  7.11 us (1%)
    all_to_all x1, blocking collectives, exchange(): return lax.all_to_all(x, axes, split_axis=0, concat_axis=0, tiled=True)  212 us
    ppermute x21, waiting for transfers between devices, shift(): lax.ppermute(x, 'row', [(p, (p + t) % row_count) for p in range(row_count)])  90.2 us
    ppermute x21, starting transfers between devices, shift(): lax.ppermute(x, 'row', [(p, (p + t) % row_count) for p in range(row_count)])  44.7 us
    pallas_call x1, Pallas kernels, eliminate(): pl.pallas_call(main_body, grid=(parts // 2,), in_specs=[SMEM, whole3, who...  36 us
    unnamed x74, local copies, waits for them, and re-layouts  32.2 us
    all_to_all x1, waiting for transfers between devices, exchange(): return lax.all_to_all(x, axes, split_axis=0, concat_axis=0, tiled=True)  29.8 us
    all_gather x1, waiting for transfers between devices, step(): gathered = lax.all_gather(mixed.reshape(-1, NB), 'col', axis=0, tiled=True)  25.7 us
    ppermute x7, waiting for transfers between devices, leave(): lax.ppermute(x, 'row', [(p, (p + t) % row_count) for p in range(STEPS)])  17 us
  transfers between devices with their start and end apart: 30, of which 14 were waited for; matrix products, arithmetic and copies ran while one was open for 2% of the time, Pallas kernels for 4%

profile of v2, /device:TPU:30, one launch (start us, length us, event | category | flops | bytes accessed | tf_op | source)
XLA Modules:
  0.0 577.3 jit_solution(18024279082040638827)
XLA Ops:
  10.7 12.0 %pick_rows.1 = (f32[48,8,128]{2,1,0:T(8,128)S(1)}, f32[48,8,128]{2,1,0:T(8,128)S(1)}, f32[48,8,128]{2,1,0:T(8,128)S(1)}, f32[48,8,128]{2,1,0:T(8,128)S(1)}, f32[...) custom-call(s32[2]{0:T(128)S(1)} %pad_add_fusion.7.me, ...), custom_call_target="tpu_custom_call" | custom-call | tf_op jit(solution)/shard_map/pick_rows/pallas_call | solution.py:122
  36.9 7.6 %collective-permute-done.11 = f32[48,8,128]{2,1,0:T(8,128)S(1)} collective-permute-done((f32[48,8,128]{2,1,0:T(8,128)S(1)}, f32[48,8,128]{2,1,0:T(8,128)S(1)}, u32[]{:S(2)}, u32[]{:S(2)}) %collective-permute-start.11) | collective-permute-done | bytes 196640 | tf_op jit(solution)/shard_map/ppermute | solution.py:457
  44.5 6.0 %collective-permute-done.12 = f32[48,8,128]{2,1,0:T(8,128)S(1)} collective-permute-done((f32[48,8,128]{2,1,0:T(8,128)S(1)}, f32[48,8,128]{2,1,0:T(8,128)S(1)}, u32[]{:S(2)}, u32[]{:S(2)}) %collective-permute-start.12) | collective-permute-done | bytes 196640 | tf_op jit(solution)/shard_map/ppermute | solution.py:457
  53.8 13.2 %conditional.1 = ((f32[2048,8,128]{2,1,0:T(8,128)}, f32[16,184,256]{2,1,0:T(8,128)})) conditional(s32[]{:T(128)} %convert_element_type.34, (s32[384]{0:T(512)S(1)}, f32[2048,8,128]{2,1,0:T(8,128)}, f32[768,256]{1,0:T(8,128)}, f32[16,8,256]{0,2,1:T(8,128)}, f32[48,8,128]{2,1,0:T(8,128)S(1)}, /*index=5*/f32[48,8,128]{2,1,0:T(8,128)S(1)}, ...), branch_computations={%region_14.15_spmd, %region_15.17_spmd} | conditional | flops 4776960 | bytes 31781156 | solution.py:495
  55.4 11.7 %branch_0_fun.1 = (f32[2048,8,128]{2,1,0:T(8,128)}, f32[16,184,256]{2,1,0:T(8,128)}) custom-call(s32[384]{0:T(512)S(1)} %get-tuple-element.79.landing, f32[2048,8,128]{2,1,0:T(8,128)} %get-tuple-element.80.rows, f32[768,256]{1,0:T(8,128)} %get-tuple-element.81.corner, f32[16,8,256]{2,1,0:T(8,128)S(1)} %copy.37.notes, ...), custom_call_target="tpu_custom_call" | custom-call | tf_op jit(solution)/shard_map/cond/branch_0_fun/pallas_call | solution.py:202
  67.1 6.9 %all-to-all-start = ((f32[16,184,256]{2,1,0:T(8,128)}), f32[16,184,256]{2,1,0:T(8,128)}, u32[]{:S(2)}, u32[]{:S(2)}) async-start(f32[16,184,256]{2,1,0:T(8,128)} %get-tuple-element.170), calls=%async_computation | async-start | bytes 6029312 | tf_op jit(solution)/shard_map/all_to_all | solution.py:451
  81.8 29.8 %all-to-all-done = f32[16,184,256]{2,1,0:T(8,128)} async-done(((f32[16,184,256]{2,1,0:T(8,128)}), f32[16,184,256]{2,1,0:T(8,128)}, u32[]{:S(2)}, u32[]{:S(2)}) %all-to-all-start) | async-done | bytes 3014688 | tf_op jit(solution)/shard_map/all_to_all | solution.py:451
  113.7 28.2 %collective-permute-start.14 = (f32[152,256]{1,0:T(8,128)S(1)}, f32[152,256]{1,0:T(8,128)}, u32[]{:S(2)}, u32[]{:S(2)}) collective-permute-start(f32[152,256]{1,0:T(8,128)S(1)} %select_maximum_fusion), channel_id=1, source_target_pairs={{0,16},{16,32},{32,48},{48,64},{64,80},{80,96},{96,112},{112,0},{1... | collective-permute-start | bytes 466952 | tf_op jit(solution)/shard_map/ppermute | solution.py:454
  144.7 9.9 %pack_tiles.1 = f32[256,128,128]{2,1,0:T(8,128)S(1)} custom-call(s32[96]{0:T(128)S(1)} %get-tuple-element.298.slot, f32[96,128,128]{2,1,0:T(8,128)S(1)} %copy-done.3), custom_call_target="tpu_custom_call" | custom-call | tf_op jit(solution)/shard_map/pack_tiles/pallas_call | solution.py:55
  154.6 5.7 copy-done
  163.2 5.7 collective-permute-done.15
  168.9 6.4 %collective-permute-done.16 = f32[152,256]{1,0:T(8,128)S(1)} collective-permute-done((f32[152,256]{1,0:T(8,128)S(1)}, f32[152,256]{1,0:T(8,128)S(1)}, u32[]{:S(2)}, u32[]{:S(2)}) %collective-permute-start.16) | collective-permute-done | bytes 155680 | tf_op jit(solution)/shard_map/ppermute | solution.py:454
  175.4 6.7 %collective-permute-done.17 = f32[152,256]{1,0:T(8,128)S(1)} collective-permute-done((f32[152,256]{1,0:T(8,128)S(1)}, f32[152,256]{1,0:T(8,128)S(1)}, u32[]{:S(2)}, u32[]{:S(2)}) %collective-permute-start.17) | collective-permute-done | bytes 155680 | tf_op jit(solution)/shard_map/ppermute | solution.py:454
  182.8 8.1 %collective-permute-done.18 = f32[152,256]{1,0:T(8,128)S(1)} collective-permute-done((f32[152,256]{1,0:T(8,128)S(1)}, f32[152,256]{1,0:T(8,128)S(1)}, u32[]{:S(2)}, u32[]{:S(2)}) %collective-permute-start.18) | collective-permute-done | bytes 155680 | tf_op jit(solution)/shard_map/ppermute | solution.py:454
  190.9 9.2 %collective-permute-done.19 = f32[152,256]{1,0:T(8,128)S(1)} collective-permute-done((f32[152,256]{1,0:T(8,128)S(1)}, f32[152,256]{1,0:T(8,128)S(1)}, u32[]{:S(2)}, u32[]{:S(2)}) %collective-permute-start.19) | collective-permute-done | bytes 155680 | tf_op jit(solution)/shard_map/ppermute | solution.py:454
  200.2 17.5 %collective-permute-done.20 = f32[152,256]{1,0:T(8,128)S(1)} collective-permute-done((f32[152,256]{1,0:T(8,128)S(1)}, f32[152,256]{1,0:T(8,128)S(1)}, u32[]{:S(2)}, u32[]{:S(2)}) %collective-permute-start.20) | collective-permute-done | bytes 155680 | tf_op jit(solution)/shard_map/ppermute | solution.py:454
  221.7 10.8 %collective-permute-done.25.refs_5_ = f32[96,8,128]{2,1,0:T(8,128)S(1)} collective-permute-done((f32[96,8,128]{2,1,0:T(8,128)}, f32[96,8,128]{2,1,0:T(8,128)S(1)}, u32[]{:S(2)}, u32[]{:S(2)}) %collective-permute-start.25) | collective-permute-done | bytes 393248 | tf_op jit(solution)/shard_map/ppermute | solution.py:454
  236.5 212.0 %all_to_all.10.received = f32[256,128,128]{2,1,0:T(8,128)} all-to-all(f32[256,128,128]{2,1,0:T(8,128)} %copy-done), channel_id=1, replica_groups=mesh['row'=8,'col'=16] {'row','col'}, dimensions={0} | all-to-all | bytes 33554432 | tf_op jit(solution)/shard_map/all_to_all | solution.py:451
  452.8 4.9 collective-permute-start.32
  460.1 21.7 %collective-permute-done.34.rest_7_ = f32[96,8,128]{2,1,0:T(8,128)S(1)} collective-permute-done((f32[96,8,128]{2,1,0:T(8,128)S(1)}, f32[96,8,128]{2,1,0:T(8,128)S(1)}, u32[]{:S(2)}, u32[]{:S(2)}) %collective-permute-start.34) | collective-permute-done | bytes 393248 | tf_op jit(solution)/shard_map/ppermute | solution.py:454
  481.9 5.9 %copy-done.1 = f32[256,128,128]{2,1,0:T(8,128)S(1)} copy-done((f32[256,128,128]{2,1,0:T(8,128)S(1)}, f32[256,128,128]{2,1,0:T(8,128)}, u32[]{:S(2)}) %copy-start.1) | copy-done | bytes 16777240
  487.7 12.4 %sum_tiles.1.tiles = f32[128,128,128]{2,1,0:T(8,128)S(1)} custom-call(s32[256]{0:T(256)S(1)} %convert_element_type.40.ids, f32[256,128,128]{2,1,0:T(8,128)S(1)} %copy-done.1), custom_call_target="tpu_custom_call" | custom-call | tf_op jit(solution)/shard_map/sum_tiles/pallas_call | solution.py:384
  505.7 25.7 %all-gather.2.cloned.1.call-done = f32[8448,256]{1,0:T(8,128)} async-done(((f32[528,256]{1,0:T(8,128)}), f32[8448,256]{1,0:T(8,128)}) %all-gather.2.cloned.1.call-update) | async-done | bytes 8650768 | tf_op jit(solution)/shard_map/all_gather | solution.py:512
  534.4 36.0 %eliminate.1 = f32[2048,8,128]{2,1,0:T(8,128)} custom-call(s32[2]{0:T(128)S(1)} %pad_add_fusion.7.me, f32[3,256,256]{2,1,0:T(8,128)S(1)} %copy-done.4, f32[3,256,256]{2,1,0:T(8,128)S(1)} %copy-done.5, f32[16,3,176,256]{3,2,1,0:T(8,128)} %bitcast.43, f32[16,3,176,256]{3,2,1,0:T(8,128)} %bitcast.44, f32[2048,8,128]{2,1,0:T(8,128)} %get-tuple-element.190.block, ...), custom_call_target="tpu_custom_call" | custom-call | tf_op jit(solution)/shard_map/eliminate/pallas_call | solution.py:311
  (184 shorter events, 61.8 us)
Async XLA Ops:
  27.9 8.9 %collective-permute-start.9 = (f32[48,8,128]{2,1,0:T(8,128)S(1)}, f32[48,8,128]{2,1,0:T(8,128)S(1)}, u32[]{:S(2)}, u32[]{:S(2)}) collective-permute-start(f32[48,8,128]{2,1,0:T(8,128)S(1)} %get-tuple-element.155), channel_id=1, source_target_pairs={{0,48},{16,64},{32,80},{1,49},{17,65},{33,81},{2,50},{18,66},{34,8... | collective-permute-start | bytes 589832 | tf_op jit(solution)/shard_map/ppermute | solution.py:457
  29.2 15.2 %collective-permute-start.11 = (f32[48,8,128]{2,1,0:T(8,128)S(1)}, f32[48,8,128]{2,1,0:T(8,128)S(1)}, u32[]{:S(2)}, u32[]{:S(2)}) collective-permute-start(f32[48,8,128]{2,1,0:T(8,128)S(1)} %get-tuple-element.157), channel_id=1, source_target_pairs={{0,80},{16,96},{32,112},{1,81},{17,97},{33,113},{2,82},{18,98},{34... | collective-permute-start | bytes 589832 | tf_op jit(solution)/shard_map/ppermute | solution.py:457
  34.2 16.3 %collective-permute-start.12 = (f32[48,8,128]{2,1,0:T(8,128)S(1)}, f32[48,8,128]{2,1,0:T(8,128)S(1)}, u32[]{:S(2)}, u32[]{:S(2)}) collective-permute-start(f32[48,8,128]{2,1,0:T(8,128)S(1)} %get-tuple-element.158), channel_id=1, source_target_pairs={{0,96},{16,112},{32,0},{1,97},{17,113},{33,1},{2,98},{18,114},{34,... | collective-permute-start | bytes 589832 | tf_op jit(solution)/shard_map/ppermute | solution.py:457
  35.5 18.3 %collective-permute-start.13 = (f32[48,8,128]{2,1,0:T(8,128)S(1)}, f32[48,8,128]{2,1,0:T(8,128)S(1)}, u32[]{:S(2)}, u32[]{:S(2)}) collective-permute-start(f32[48,8,128]{2,1,0:T(8,128)S(1)} %get-tuple-element.159), channel_id=1, source_target_pairs={{0,112},{16,0},{32,16},{1,113},{17,1},{33,17},{2,114},{18,2},{34,1... | collective-permute-start | bytes 589832 | tf_op jit(solution)/shard_map/ppermute | solution.py:457
  67.1 44.5 %all-to-all-start = ((f32[16,184,256]{2,1,0:T(8,128)}), f32[16,184,256]{2,1,0:T(8,128)}, u32[]{:S(2)}, u32[]{:S(2)}) async-start(f32[16,184,256]{2,1,0:T(8,128)} %get-tuple-element.170), calls=%async_computation | async-start | bytes 6029312 | tf_op jit(solution)/shard_map/all_to_all | solution.py:451
  74.0 457.4 %all-gather.2.cloned.1.call-start = ((), (), s32[]{:S(2)}) async-start(), calls=%async_computation.2 | async-start | bytes 9191424 | tf_op jit(solution)/shard_map/all_gather | solution.py:512
  74.1 143.7 %collective-permute-start.21 = (f32[96,8,128]{2,1,0:T(8,128)S(1)}, f32[96,8,128]{2,1,0:T(8,128)S(1)}, u32[]{:S(2)}, u32[]{:S(2)}) collective-permute-start(f32[96,8,128]{2,1,0:T(8,128)S(1)} %copy-done.29), channel_id=1, source_target_pairs={{0,16},{16,32},{32,48},{48,64},{64,80},{80,96},{96,112},{112,0},{1... | collective-permute-start | bytes 1179656 | tf_op jit(solution)/shard_map/ppermute | solution.py:454
  77.9 140.0 %collective-permute-start.22 = (f32[96,8,128]{2,1,0:T(8,128)S(1)}, f32[96,8,128]{2,1,0:T(8,128)S(1)}, u32[]{:S(2)}, u32[]{:S(2)}) collective-permute-start(f32[96,8,128]{2,1,0:T(8,128)S(1)} %copy-done.27), channel_id=1, source_target_pairs={{0,32},{16,48},{32,64},{48,80},{64,96},{80,112},{96,0},{112,16},{1... | collective-permute-start | bytes 1179656 | tf_op jit(solution)/shard_map/ppermute | solution.py:454
  77.9 143.9 %collective-permute-start.23 = (f32[96,8,128]{2,1,0:T(8,128)}, f32[96,8,128]{2,1,0:T(8,128)S(1)}, u32[]{:S(2)}, u32[]{:S(2)}) collective-permute-start(f32[96,8,128]{2,1,0:T(8,128)} %get-tuple-element.174), channel_id=1, source_target_pairs={{0,48},{16,64},{32,80},{48,96},{64,112},{80,0},{96,16},{112,32},{1... | collective-permute-start | bytes 1179656 | tf_op jit(solution)/shard_map/ppermute | solution.py:454
  77.9 143.9 %collective-permute-start.24 = (f32[96,8,128]{2,1,0:T(8,128)}, f32[96,8,128]{2,1,0:T(8,128)S(1)}, u32[]{:S(2)}, u32[]{:S(2)}) collective-permute-start(f32[96,8,128]{2,1,0:T(8,128)} %get-tuple-element.175), channel_id=1, source_target_pairs={{0,64},{16,80},{32,96},{48,112},{64,0},{80,16},{96,32},{112,48},{1... | collective-permute-start | bytes 1179656 | tf_op jit(solution)/shard_map/ppermute | solution.py:454
  113.7 48.4 %collective-permute-start.14 = (f32[152,256]{1,0:T(8,128)S(1)}, f32[152,256]{1,0:T(8,128)}, u32[]{:S(2)}, u32[]{:S(2)}) collective-permute-start(f32[152,256]{1,0:T(8,128)S(1)} %select_maximum_fusion), channel_id=1, source_target_pairs={{0,16},{16,32},{32,48},{48,64},{64,80},{80,96},{96,112},{112,0},{1... | collective-permute-start | bytes 466952 | tf_op jit(solution)/shard_map/ppermute | solution.py:454
  182.1 8.8 %collective-permute-start.18 = (f32[152,256]{1,0:T(8,128)S(1)}, f32[152,256]{1,0:T(8,128)S(1)}, u32[]{:S(2)}, u32[]{:S(2)}) collective-permute-start(f32[152,256]{1,0:T(8,128)S(1)} %select_maximum_fusion), channel_id=1, source_target_pairs={{0,80},{16,96},{32,112},{48,0},{64,16},{80,32},{96,48},{112,64},{1... | collective-permute-start | bytes 466952 | tf_op jit(solution)/shard_map/ppermute | solution.py:454
  190.9 9.2 %collective-permute-start.19 = (f32[152,256]{1,0:T(8,128)S(1)}, f32[152,256]{1,0:T(8,128)S(1)}, u32[]{:S(2)}, u32[]{:S(2)}) collective-permute-start(f32[152,256]{1,0:T(8,128)S(1)} %select_maximum_fusion), channel_id=1, source_target_pairs={{0,96},{16,112},{32,0},{48,16},{64,32},{80,48},{96,64},{112,80},{1... | collective-permute-start | bytes 466952 | tf_op jit(solution)/shard_map/ppermute | solution.py:454
  200.2 17.5 %collective-permute-start.20 = (f32[152,256]{1,0:T(8,128)S(1)}, f32[152,256]{1,0:T(8,128)S(1)}, u32[]{:S(2)}, u32[]{:S(2)}) collective-permute-start(f32[152,256]{1,0:T(8,128)S(1)} %select_maximum_fusion), channel_id=1, source_target_pairs={{0,112},{16,0},{32,16},{48,32},{64,48},{80,64},{96,80},{112,96},{1... | collective-permute-start | bytes 466952 | tf_op jit(solution)/shard_map/ppermute | solution.py:454
  217.7 14.9 %collective-permute-start.25 = (f32[96,8,128]{2,1,0:T(8,128)}, f32[96,8,128]{2,1,0:T(8,128)S(1)}, u32[]{:S(2)}, u32[]{:S(2)}) collective-permute-start(f32[96,8,128]{2,1,0:T(8,128)} %get-tuple-element.176), channel_id=1, source_target_pairs={{0,80},{16,96},{32,112},{48,0},{64,16},{80,32},{96,48},{112,64},{1... | collective-permute-start | bytes 1179656 | tf_op jit(solution)/shard_map/ppermute | solution.py:454
  217.8 14.8 %collective-permute-start.26 = (f32[96,8,128]{2,1,0:T(8,128)S(1)}, f32[96,8,128]{2,1,0:T(8,128)S(1)}, u32[]{:S(2)}, u32[]{:S(2)}) collective-permute-start(f32[96,8,128]{2,1,0:T(8,128)S(1)} %copy-done.25), channel_id=1, source_target_pairs={{0,96},{16,112},{32,0},{48,16},{64,32},{80,48},{96,64},{112,80},{1... | collective-permute-start | bytes 1179656 | tf_op jit(solution)/shard_map/ppermute | solution.py:454
  217.9 18.6 %collective-permute-start.27 = (f32[96,8,128]{2,1,0:T(8,128)S(1)}, f32[96,8,128]{2,1,0:T(8,128)S(1)}, u32[]{:S(2)}, u32[]{:S(2)}) collective-permute-start(f32[96,8,128]{2,1,0:T(8,128)S(1)} %copy-done.23), channel_id=1, source_target_pairs={{0,112},{16,0},{32,16},{48,32},{64,48},{80,64},{96,80},{112,96},{1... | collective-permute-start | bytes 1179656 | tf_op jit(solution)/shard_map/ppermute | solution.py:454
  452.7 29.2 %collective-permute-start.34 = (f32[96,8,128]{2,1,0:T(8,128)S(1)}, f32[96,8,128]{2,1,0:T(8,128)S(1)}, u32[]{:S(2)}, u32[]{:S(2)}) collective-permute-start(f32[96,8,128]{2,1,0:T(8,128)S(1)} %collect_rows.1.rest_0_), channel_id=1, source_target_pairs={{0,112},{16,0},{32,16},{48,32},{64,48},{80,64},{96,80},{112,96},{1... | collective-permute-start | bytes 1179656 | tf_op jit(solution)/shard_map/ppermute | solution.py:454
  452.8 29.1 %collective-permute-start.33 = (f32[96,8,128]{2,1,0:T(8,128)S(1)}, f32[96,8,128]{2,1,0:T(8,128)S(1)}, u32[]{:S(2)}, u32[]{:S(2)}) collective-permute-start(f32[96,8,128]{2,1,0:T(8,128)S(1)} %collect_rows.1.rest_0_), channel_id=1, source_target_pairs={{0,96},{16,112},{32,0},{48,16},{64,32},{80,48},{96,64},{112,80},{1... | collective-permute-start | bytes 1179656 | tf_op jit(solution)/shard_map/ppermute | solution.py:454
  452.8 50.5 %collective-permute-start.32 = (f32[96,8,128]{2,1,0:T(8,128)S(1)}, f32[96,8,128]{2,1,0:T(8,128)S(1)}, u32[]{:S(2)}, u32[]{:S(2)}) collective-permute-start(f32[96,8,128]{2,1,0:T(8,128)S(1)} %collect_rows.1.rest_0_), channel_id=1, source_target_pairs={{0,80},{16,96},{32,112},{48,0},{64,16},{80,32},{96,48},{112,64},{1... | collective-permute-start | bytes 1179656 | tf_op jit(solution)/shard_map/ppermute | solution.py:454
  457.7 45.7 %collective-permute-start.31 = (f32[96,8,128]{2,1,0:T(8,128)S(1)}, f32[96,8,128]{2,1,0:T(8,128)S(1)}, u32[]{:S(2)}, u32[]{:S(2)}) collective-permute-start(f32[96,8,128]{2,1,0:T(8,128)S(1)} %collect_rows.1.rest_0_), channel_id=1, source_target_pairs={{0,64},{16,80},{32,96},{48,112},{64,0},{80,16},{96,32},{112,48},{1... | collective-permute-start | bytes 1179656 | tf_op jit(solution)/shard_map/ppermute | solution.py:454
  458.9 44.4 %collective-permute-start.30 = (f32[96,8,128]{2,1,0:T(8,128)S(1)}, f32[96,8,128]{2,1,0:T(8,128)S(1)}, u32[]{:S(2)}, u32[]{:S(2)}) collective-permute-start(f32[96,8,128]{2,1,0:T(8,128)S(1)} %collect_rows.1.rest_0_), channel_id=1, source_target_pairs={{0,48},{16,64},{32,80},{48,96},{64,112},{80,0},{96,16},{112,32},{1... | collective-permute-start | bytes 1179656 | tf_op jit(solution)/shard_map/ppermute | solution.py:454
  481.8 22.3 %collective-permute-start.29 = (f32[96,8,128]{2,1,0:T(8,128)S(1)}, f32[96,8,128]{2,1,0:T(8,128)S(1)}, u32[]{:S(2)}, u32[]{:S(2)}) collective-permute-start(f32[96,8,128]{2,1,0:T(8,128)S(1)} %collect_rows.1.rest_0_), channel_id=1, source_target_pairs={{0,32},{16,48},{32,64},{48,80},{64,96},{80,112},{96,0},{112,16},{1... | collective-permute-start | bytes 1179656 | tf_op jit(solution)/shard_map/ppermute | solution.py:454
  481.8 23.1 %collective-permute-start.28 = (f32[96,8,128]{2,1,0:T(8,128)S(1)}, f32[96,8,128]{2,1,0:T(8,128)S(1)}, u32[]{:S(2)}, u32[]{:S(2)}) collective-permute-start(f32[96,8,128]{2,1,0:T(8,128)S(1)} %collect_rows.1.rest_0_), channel_id=1, source_target_pairs={{0,16},{16,32},{32,48},{48,64},{64,80},{80,96},{96,112},{112,0},{1... | collective-permute-start | bytes 1179656 | tf_op jit(solution)/shard_map/ppermute | solution.py:454
  (40 other events, 1487.1 us)
Sparse Core Ops, SparseCore 0:
  448.6 82.7 all-gather.1

commit v3 on v2

--- a/solution.py
+++ b/solution.py
@@ -62,7 +62,7 @@
             pltpu.SemaphoreType.DMA(()),
             pltpu.SemaphoreType.DMA(()),
         ],
-        compiler_params=room(10),
+        compiler_params=room(60),
         name="pack_tiles",
     )(slot, tiles)
 
@@ -393,7 +393,7 @@
             pltpu.SemaphoreType.DMA((RING,)),
             pltpu.SemaphoreType.DMA(()),
         ],
-        compiler_params=room(14),
+        compiler_params=room(60),
         name="sum_tiles",
     )(ids, received)
 
@@ -499,6 +499,8 @@
     notes = dealt[:, -8, : row_count * CAP].reshape(col_count, row_count, CAP).transpose(1, 0, 2)
     notes = jnp.pad(notes.reshape(1, -1), ((0, 7), (0, NB - notes.size)))
     partial = jnp.concatenate([partial, notes])
+    summed = collect(given)
+    chunks = [summed] + [shift(summed, t) for t in range(1, row_count)]
     partial = jnp.stack([partial] + [shift(partial, t) for t in range(1, row_count)])
     corner = jnp.sum(partial[:, :-8], axis=0).reshape(STEPS, -1, NB)
     mixed = jnp.concatenate([dealt[:STEPS, :tall], corner], axis=1)
@@ -506,13 +508,11 @@
     notes = lax.dynamic_slice_in_dim(notes, row_place * col_count * CAP, col_count * CAP, 1)
     turn = (row_place - jnp.arange(row_count, dtype=I32)) % row_count
     ids_in = notes[turn].reshape(-1).astype(I32)
-    send, mixed, ids_in, *given = lax.optimization_barrier((send, mixed, ids_in, *given))
+    send, mixed, ids_in, *chunks = lax.optimization_barrier((send, mixed, ids_in, *chunks))
     received = exchange(send, ("row", "col"))
-    received, mixed, *given = lax.optimization_barrier((received, mixed, *given))
+    received, mixed = lax.optimization_barrier((received, mixed))
     gathered = lax.all_gather(mixed.reshape(-1, NB), "col", axis=0, tiled=True)
     gathered = gathered.reshape(col_count, STEPS, -1, NB)
-    summed = collect(given)
-    chunks = [summed] + [shift(summed, t) for t in range(1, row_count)]
     tiles = sum_tiles(ids_in, received, local_rows // LANES * GROUPS)
     out = eliminate(me, l_inverse, u_inverse, gathered, moved, tiles, chunks)
     return out.reshape(-1).reshape(front_matrix.shape)

time: 585 us -> 562 us (0.961)
  local copies, waits for them, and re-layouts: 40.5 us -> 17.3 us
  waiting for transfers between devices: 163 us -> 174 us
    unnamed x74 -> x52, local copies, waits for them, and re-layouts: 32.2 us -> 8.7 us
    all_gather x1, waiting for transfers between devices: 25.7 us -> 42.8 us  [step(): gathered = lax.all_gather(mixed.reshape(-1, NB), 'col', axis=0, tiled=True)]
    ppermute x21, waiting for transfers between devices: 90.2 us -> 79.2 us  [shift(): lax.ppermute(x, 'row', [(p, (p + t) % row_count) for p in range(row_count)])]
    ppermute x21, starting transfers between devices: 44.7 us -> 36.7 us  [shift(): lax.ppermute(x, 'row', [(p, (p + t) % row_count) for p in range(row_count)])]
    all_to_all x1, waiting for transfers between devices: 29.8 us -> 36.3 us  [exchange(): return lax.all_to_all(x, axes, split_axis=0, concat_axis=0, tiled=True)]
  transfers between devices with their start and end apart: 30 -> 30, of which waited for: 14 -> 14; matrix products, arithmetic and copies ran while one was open for 2% -> 3% of each run, Pallas kernels for 4% -> 3%
where the time goes in v3:
time: 562 us; the launch traced here: 559 us
  blocking collectives  214 us (38%)
  waiting for transfers between devices  174 us (31%)
  Pallas kernels  77 us (14%)
  starting transfers between devices  52.9 us (9%)
  local copies, waits for them, and re-layouts  17.3 us (3%)
  between operations  14.7 us (3%)
  other arithmetic  9.39 us (2%)
    all_to_all x1, blocking collectives, exchange(): return lax.all_to_all(x, axes, split_axis=0, concat_axis=0, tiled=True)  214 us
    ppermute x21, waiting for transfers between devices, shift(): lax.ppermute(x, 'row', [(p, (p + t) % row_count) for p in range(row_count)])  79.2 us
    all_gather x1, waiting for transfers between devices, step(): gathered = lax.all_gather(mixed.reshape(-1, NB), 'col', axis=0, tiled=True)  42.8 us
    ppermute x21, starting transfers between devices, shift(): lax.ppermute(x, 'row', [(p, (p + t) % row_count) for p in range(row_count)])  36.7 us
    all_to_all x1, waiting for transfers between devices, exchange(): return lax.all_to_all(x, axes, split_axis=0, concat_axis=0, tiled=True)  36.3 us
    pallas_call x1, Pallas kernels, eliminate(): pl.pallas_call(main_body, grid=(parts // 2,), in_specs=[SMEM, whole3, who...  36.1 us
    ppermute x7, waiting for transfers between devices, leave(): lax.ppermute(x, 'row', [(p, (p + t) % row_count) for p in range(STEPS)])  15.4 us
    pallas_call x1, Pallas kernels, land_rows(): pl.pallas_call(land_body, in_specs=[SMEM, ANY, vmem, vmem] + [vmem] * len...  11.8 us
  transfers between devices with their start and end apart: 30, of which 14 were waited for; matrix products, arithmetic and copies ran while one was open for 3% of the time, Pallas kernels for 3%

profile of v3, /device:TPU:30, one launch (start us, length us, event | category | flops | bytes accessed | tf_op | source)
XLA Modules:
  0.0 558.9 jit_solution(13212205254771941445)
XLA Ops:
  10.7 11.8 %pick_rows.1 = (f32[48,8,128]{2,1,0:T(8,128)S(1)}, f32[48,8,128]{2,1,0:T(8,128)S(1)}, f32[48,8,128]{2,1,0:T(8,128)S(1)}, f32[48,8,128]{2,1,0:T(8,128)S(1)}, f32[...) custom-call(s32[2]{0:T(128)S(1)} %pad_add_fusion.7.me, ...), custom_call_target="tpu_custom_call" | custom-call | tf_op jit(solution)/shard_map/pick_rows/pallas_call | solution.py:122
  38.7 5.5 collective-permute-done.11
  44.2 5.8 %collective-permute-done.12 = f32[48,8,128]{2,1,0:T(8,128)S(1)} collective-permute-done((f32[48,8,128]{2,1,0:T(8,128)S(1)}, f32[48,8,128]{2,1,0:T(8,128)S(1)}, u32[]{:S(2)}, u32[]{:S(2)}) %collective-permute-start.12) | collective-permute-done | bytes 196640 | tf_op jit(solution)/shard_map/ppermute | solution.py:457
  54.1 12.1 %conditional.1 = ((f32[2048,8,128]{2,1,0:T(8,128)}, f32[16,184,256]{2,1,0:T(8,128)})) conditional(s32[]{:T(128)} %convert_element_type.34, (s32[384]{0:T(512)S(1)}, f32[2048,8,128]{2,1,0:T(8,128)}, f32[768,256]{1,0:T(8,128)S(1)}, f32[16,8,256]{0,2,1:T(8,128)S(1)}, f32[48,8,128]{2,1,0:T(8,128)S(1)}, /*index=5*/f32[48,8,128]{2,1,0:T(8,128)}, ...), branch_computations={%region_14.15_spmd, %region_15.17_spmd} | conditional | flops 4776960 | bytes 35451228 | solution.py:495
  54.4 11.8 %branch_0_fun.1 = (f32[2048,8,128]{2,1,0:T(8,128)}, f32[16,184,256]{2,1,0:T(8,128)}) custom-call(s32[384]{0:T(512)S(1)} %get-tuple-element.79.landing, f32[2048,8,128]{2,1,0:T(8,128)} %get-tuple-element.80.rows, f32[768,256]{1,0:T(8,128)S(1)} %get-tuple-element.81.corner, f32[16,8,256]{2,1,0:T(8,128)S(1)} %copy.37.notes, ...), custom_call_target="tpu_custom_call" | custom-call | tf_op jit(solution)/shard_map/cond/branch_0_fun/pallas_call | solution.py:202
  66.3 6.9 %all-to-all-start = ((f32[16,184,256]{2,1,0:T(8,128)}), f32[16,184,256]{2,1,0:T(8,128)}, u32[]{:S(2)}, u32[]{:S(2)}) async-start(f32[16,184,256]{2,1,0:T(8,128)} %get-tuple-element.162), calls=%async_computation | async-start | bytes 6029312 | tf_op jit(solution)/shard_map/all_to_all | solution.py:451
  73.3 4.5 collective-permute-start.21
  82.4 16.8 %collective-permute-done.21.refs_1_ = f32[96,8,128]{2,1,0:T(8,128)S(1)} collective-permute-done((f32[96,8,128]{2,1,0:T(8,128)S(1)}, f32[96,8,128]{2,1,0:T(8,128)S(1)}, u32[]{:S(2)}, u32[]{:S(2)}) %collective-permute-start.21) | collective-permute-done | bytes 393248 | tf_op jit(solution)/shard_map/ppermute | solution.py:454
  99.8 36.3 %all-to-all-done = f32[16,184,256]{2,1,0:T(8,128)} async-done(((f32[16,184,256]{2,1,0:T(8,128)}), f32[16,184,256]{2,1,0:T(8,128)}, u32[]{:S(2)}, u32[]{:S(2)}) %all-to-all-start) | async-done | bytes 3014688 | tf_op jit(solution)/shard_map/all_to_all | solution.py:451
  144.6 6.2 %pack_tiles.1 = f32[256,128,128]{2,1,0:T(8,128)} custom-call(s32[96]{0:T(128)} %get-tuple-element.282.slot, f32[96,128,128]{2,1,0:T(8,128)} %tiles.1), custom_call_target="tpu_custom_call" | custom-call | tf_op jit(solution)/shard_map/pack_tiles/pallas_call | solution.py:55
  158.4 5.4 collective-permute-start.15
  164.7 10.9 %collective-permute-done.15 = f32[152,256]{1,0:T(8,128)S(1)} collective-permute-done((f32[152,256]{1,0:T(8,128)}, f32[152,256]{1,0:T(8,128)S(1)}, u32[]{:S(2)}, u32[]{:S(2)}) %collective-permute-start.15) | collective-permute-done | bytes 155680 | tf_op jit(solution)/shard_map/ppermute | solution.py:454
  175.6 9.1 %collective-permute-start.16 = (f32[152,256]{1,0:T(8,128)}, f32[152,256]{1,0:T(8,128)S(1)}, u32[]{:S(2)}, u32[]{:S(2)}) collective-permute-start(f32[152,256]{1,0:T(8,128)} %select_maximum_fusion), channel_id=1, source_target_pairs={{0,48},{16,64},{32,80},{48,96},{64,112},{80,0},{96,16},{112,32},{1... | collective-permute-start | bytes 466952 | tf_op jit(solution)/shard_map/ppermute | solution.py:454
  184.8 6.4 %collective-permute-done.16 = f32[152,256]{1,0:T(8,128)S(1)} collective-permute-done((f32[152,256]{1,0:T(8,128)}, f32[152,256]{1,0:T(8,128)S(1)}, u32[]{:S(2)}, u32[]{:S(2)}) %collective-permute-start.16) | collective-permute-done | bytes 155680 | tf_op jit(solution)/shard_map/ppermute | solution.py:454
  191.2 6.9 %collective-permute-done.17 = f32[152,256]{1,0:T(8,128)S(1)} collective-permute-done((f32[152,256]{1,0:T(8,128)}, f32[152,256]{1,0:T(8,128)S(1)}, u32[]{:S(2)}, u32[]{:S(2)}) %collective-permute-start.17) | collective-permute-done | bytes 155680 | tf_op jit(solution)/shard_map/ppermute | solution.py:454
  202.6 4.8 collective-permute-done.18
  207.3 9.4 %collective-permute-done.19 = f32[152,256]{1,0:T(8,128)S(1)} collective-permute-done((f32[152,256]{1,0:T(8,128)}, f32[152,256]{1,0:T(8,128)S(1)}, u32[]{:S(2)}, u32[]{:S(2)}) %collective-permute-start.19) | collective-permute-done | bytes 155680 | tf_op jit(solution)/shard_map/ppermute | solution.py:454
  216.7 14.7 %collective-permute-done.20 = f32[152,256]{1,0:T(8,128)S(1)} collective-permute-done((f32[152,256]{1,0:T(8,128)}, f32[152,256]{1,0:T(8,128)S(1)}, u32[]{:S(2)}, u32[]{:S(2)}) %collective-permute-start.20) | collective-permute-done | bytes 155680 | tf_op jit(solution)/shard_map/ppermute | solution.py:454
  236.0 4.5 collective-permute-done.30.rest_3_
  240.5 4.8 collective-permute-done.29.rest_2_
  245.2 213.9 %all_to_all.10.received = f32[256,128,128]{2,1,0:T(8,128)} all-to-all(f32[256,128,128]{2,1,0:T(8,128)} %pack_tiles.1), channel_id=1, replica_groups=mesh['row'=8,'col'=16] {'row','col'}, dimensions={0} | all-to-all | bytes 33554432 | tf_op jit(solution)/shard_map/all_to_all | solution.py:451
  459.3 10.9 %sum_tiles.1.tiles = f32[128,128,128]{2,1,0:T(8,128)} custom-call(s32[256]{0:T(256)} %convert_element_type.40.ids, f32[256,128,128]{2,1,0:T(8,128)} %all_to_all.10.received), custom_call_target="tpu_custom_call" | custom-call | tf_op jit(solution)/shard_map/sum_tiles/pallas_call | solution.py:384
  470.1 42.8 %all-gather.2.cloned.1.call-done = f32[8448,256]{1,0:T(8,128)} async-done(((f32[528,256]{1,0:T(8,128)}), f32[8448,256]{1,0:T(8,128)}) %all-gather.2.cloned.1.call-update) | async-done | bytes 8650768 | tf_op jit(solution)/shard_map/all_gather | solution.py:514
  515.9 36.1 %eliminate.1 = f32[2048,8,128]{2,1,0:T(8,128)} custom-call(s32[2]{0:T(128)S(1)} %pad_add_fusion.7.me, f32[3,256,256]{2,1,0:T(8,128)S(1)} %copy-done, f32[3,256,256]{2,1,0:T(8,128)S(1)} %copy-done.1, f32[16,3,176,256]{3,2,1,0:T(8,128)} %bitcast.43, f32[16,3,176,256]{3,2,1,0:T(8,128)} %bitcast.44, f32[2048,8,128]{2,1,0:T(8,128)} %get-tuple-element.174.block, ...), custom_call_target="tpu_custom_call" | custom-call | tf_op jit(solution)/shard_map/eliminate/pallas_call | solution.py:311
  (162 shorter events, 58.1 us)
Async XLA Ops:
  26.2 9.8 %collective-permute-start.7 = (f32[48,8,128]{2,1,0:T(8,128)S(1)}, f32[48,8,128]{2,1,0:T(8,128)}, u32[]{:S(2)}, u32[]{:S(2)}) collective-permute-start(f32[48,8,128]{2,1,0:T(8,128)S(1)} %get-tuple-element.145), channel_id=1, source_target_pairs={{0,16},{16,32},{32,48},{1,17},{17,33},{33,49},{2,18},{18,34},{34,5... | collective-permute-start | bytes 589832 | tf_op jit(solution)/shard_map/ppermute | solution.py:457
  27.5 9.8 %collective-permute-start.8 = (f32[48,8,128]{2,1,0:T(8,128)S(1)}, f32[48,8,128]{2,1,0:T(8,128)}, u32[]{:S(2)}, u32[]{:S(2)}) collective-permute-start(f32[48,8,128]{2,1,0:T(8,128)S(1)} %get-tuple-element.146), channel_id=1, source_target_pairs={{0,32},{16,48},{32,64},{1,33},{17,49},{33,65},{2,34},{18,50},{34,6... | collective-permute-start | bytes 589832 | tf_op jit(solution)/shard_map/ppermute | solution.py:457
  31.5 12.6 %collective-permute-start.11 = (f32[48,8,128]{2,1,0:T(8,128)S(1)}, f32[48,8,128]{2,1,0:T(8,128)}, u32[]{:S(2)}, u32[]{:S(2)}) collective-permute-start(f32[48,8,128]{2,1,0:T(8,128)S(1)} %get-tuple-element.149), channel_id=1, source_target_pairs={{0,80},{16,96},{32,112},{1,81},{17,97},{33,113},{2,82},{18,98},{34... | collective-permute-start | bytes 589832 | tf_op jit(solution)/shard_map/ppermute | solution.py:457
  36.0 13.9 %collective-permute-start.12 = (f32[48,8,128]{2,1,0:T(8,128)S(1)}, f32[48,8,128]{2,1,0:T(8,128)S(1)}, u32[]{:S(2)}, u32[]{:S(2)}) collective-permute-start(f32[48,8,128]{2,1,0:T(8,128)S(1)} %get-tuple-element.150), channel_id=1, source_target_pairs={{0,96},{16,112},{32,0},{1,97},{17,113},{33,1},{2,98},{18,114},{34,... | collective-permute-start | bytes 589832 | tf_op jit(solution)/shard_map/ppermute | solution.py:457
  37.4 16.8 %collective-permute-start.13 = (f32[48,8,128]{2,1,0:T(8,128)S(1)}, f32[48,8,128]{2,1,0:T(8,128)S(1)}, u32[]{:S(2)}, u32[]{:S(2)}) collective-permute-start(f32[48,8,128]{2,1,0:T(8,128)S(1)} %get-tuple-element.151), channel_id=1, source_target_pairs={{0,112},{16,0},{32,16},{1,113},{17,1},{33,17},{2,114},{18,2},{34,1... | collective-permute-start | bytes 589832 | tf_op jit(solution)/shard_map/ppermute | solution.py:457
  66.3 69.8 %all-to-all-start = ((f32[16,184,256]{2,1,0:T(8,128)}), f32[16,184,256]{2,1,0:T(8,128)}, u32[]{:S(2)}, u32[]{:S(2)}) async-start(f32[16,184,256]{2,1,0:T(8,128)} %get-tuple-element.162), calls=%async_computation | async-start | bytes 6029312 | tf_op jit(solution)/shard_map/all_to_all | solution.py:451
  73.3 439.7 %all-gather.2.cloned.1.call-start = ((), (), s32[]{:S(2)}) async-start(), calls=%async_computation.2 | async-start | bytes 9191424 | tf_op jit(solution)/shard_map/all_gather | solution.py:514
  73.3 25.9 %collective-permute-start.21 = (f32[96,8,128]{2,1,0:T(8,128)S(1)}, f32[96,8,128]{2,1,0:T(8,128)S(1)}, u32[]{:S(2)}, u32[]{:S(2)}) collective-permute-start(f32[96,8,128]{2,1,0:T(8,128)S(1)} %copy-done.17), channel_id=1, source_target_pairs={{0,16},{16,32},{32,48},{48,64},{64,80},{80,96},{96,112},{112,0},{1... | collective-permute-start | bytes 1179656 | tf_op jit(solution)/shard_map/ppermute | solution.py:454
  77.8 21.4 %collective-permute-start.22 = (f32[96,8,128]{2,1,0:T(8,128)S(1)}, f32[96,8,128]{2,1,0:T(8,128)S(1)}, u32[]{:S(2)}, u32[]{:S(2)}) collective-permute-start(f32[96,8,128]{2,1,0:T(8,128)S(1)} %copy-done.15), channel_id=1, source_target_pairs={{0,32},{16,48},{32,64},{48,80},{64,96},{80,112},{96,0},{112,16},{1... | collective-permute-start | bytes 1179656 | tf_op jit(solution)/shard_map/ppermute | solution.py:454
  78.1 63.6 %collective-permute-start.23 = (f32[96,8,128]{2,1,0:T(8,128)}, f32[96,8,128]{2,1,0:T(8,128)S(1)}, u32[]{:S(2)}, u32[]{:S(2)}) collective-permute-start(f32[96,8,128]{2,1,0:T(8,128)} %get-tuple-element.166), channel_id=1, source_target_pairs={{0,48},{16,64},{32,80},{48,96},{64,112},{80,0},{96,16},{112,32},{1... | collective-permute-start | bytes 1179656 | tf_op jit(solution)/shard_map/ppermute | solution.py:454
  78.1 72.7 %collective-permute-start.24 = (f32[96,8,128]{2,1,0:T(8,128)}, f32[96,8,128]{2,1,0:T(8,128)S(1)}, u32[]{:S(2)}, u32[]{:S(2)}) collective-permute-start(f32[96,8,128]{2,1,0:T(8,128)} %get-tuple-element.167), channel_id=1, source_target_pairs={{0,64},{16,80},{32,96},{48,112},{64,0},{80,16},{96,32},{112,48},{1... | collective-permute-start | bytes 1179656 | tf_op jit(solution)/shard_map/ppermute | solution.py:454
  82.4 68.4 %collective-permute-start.25 = (f32[96,8,128]{2,1,0:T(8,128)}, f32[96,8,128]{2,1,0:T(8,128)S(1)}, u32[]{:S(2)}, u32[]{:S(2)}) collective-permute-start(f32[96,8,128]{2,1,0:T(8,128)} %get-tuple-element.168), channel_id=1, source_target_pairs={{0,80},{16,96},{32,112},{48,0},{64,16},{80,32},{96,48},{112,64},{1... | collective-permute-start | bytes 1179656 | tf_op jit(solution)/shard_map/ppermute | solution.py:454
  99.2 51.6 %collective-permute-start.26 = (f32[96,8,128]{2,1,0:T(8,128)S(1)}, f32[96,8,128]{2,1,0:T(8,128)S(1)}, u32[]{:S(2)}, u32[]{:S(2)}) collective-permute-start(f32[96,8,128]{2,1,0:T(8,128)S(1)} %copy-done.13), channel_id=1, source_target_pairs={{0,96},{16,112},{32,0},{48,16},{64,32},{80,48},{96,64},{112,80},{1... | collective-permute-start | bytes 1179656 | tf_op jit(solution)/shard_map/ppermute | solution.py:454
  99.2 51.6 %collective-permute-start.27 = (f32[96,8,128]{2,1,0:T(8,128)S(1)}, f32[96,8,128]{2,1,0:T(8,128)S(1)}, u32[]{:S(2)}, u32[]{:S(2)}) collective-permute-start(f32[96,8,128]{2,1,0:T(8,128)S(1)} %copy-done.11), channel_id=1, source_target_pairs={{0,112},{16,0},{32,16},{48,32},{64,48},{80,64},{96,80},{112,96},{1... | collective-permute-start | bytes 1179656 | tf_op jit(solution)/shard_map/ppermute | solution.py:454
  141.7 16.7 %collective-permute-start.14 = (f32[152,256]{1,0:T(8,128)}, f32[152,256]{1,0:T(8,128)}, u32[]{:S(2)}, u32[]{:S(2)}) collective-permute-start(f32[152,256]{1,0:T(8,128)} %select_maximum_fusion), channel_id=1, source_target_pairs={{0,16},{16,32},{32,48},{48,64},{64,80},{80,96},{96,112},{112,0},{1... | collective-permute-start | bytes 466952 | tf_op jit(solution)/shard_map/ppermute | solution.py:454
  151.0 80.5 %collective-permute-start.34 = (f32[96,8,128]{2,1,0:T(8,128)S(1)}, f32[96,8,128]{2,1,0:T(8,128)S(1)}, u32[]{:S(2)}, u32[]{:S(2)}) collective-permute-start(f32[96,8,128]{2,1,0:T(8,128)S(1)} %collect_rows.1.rest_0_), channel_id=1, source_target_pairs={{0,112},{16,0},{32,16},{48,32},{64,48},{80,64},{96,80},{112,96},{1... | collective-permute-start | bytes 1179656 | tf_op jit(solution)/shard_map/ppermute | solution.py:454
  151.1 80.5 %collective-permute-start.33 = (f32[96,8,128]{2,1,0:T(8,128)S(1)}, f32[96,8,128]{2,1,0:T(8,128)S(1)}, u32[]{:S(2)}, u32[]{:S(2)}) collective-permute-start(f32[96,8,128]{2,1,0:T(8,128)S(1)} %collect_rows.1.rest_0_), channel_id=1, source_target_pairs={{0,96},{16,112},{32,0},{48,16},{64,32},{80,48},{96,64},{112,80},{1... | collective-permute-start | bytes 1179656 | tf_op jit(solution)/shard_map/ppermute | solution.py:454
  151.2 84.8 %collective-permute-start.32 = (f32[96,8,128]{2,1,0:T(8,128)S(1)}, f32[96,8,128]{2,1,0:T(8,128)S(1)}, u32[]{:S(2)}, u32[]{:S(2)}) collective-permute-start(f32[96,8,128]{2,1,0:T(8,128)S(1)} %collect_rows.1.rest_0_), channel_id=1, source_target_pairs={{0,80},{16,96},{32,112},{48,0},{64,16},{80,32},{96,48},{112,64},{1... | collective-permute-start | bytes 1179656 | tf_op jit(solution)/shard_map/ppermute | solution.py:454
  155.4 80.6 %collective-permute-start.31 = (f32[96,8,128]{2,1,0:T(8,128)S(1)}, f32[96,8,128]{2,1,0:T(8,128)S(1)}, u32[]{:S(2)}, u32[]{:S(2)}) collective-permute-start(f32[96,8,128]{2,1,0:T(8,128)S(1)} %collect_rows.1.rest_0_), channel_id=1, source_target_pairs={{0,64},{16,80},{32,96},{48,112},{64,0},{80,16},{96,32},{112,48},{1... | collective-permute-start | bytes 1179656 | tf_op jit(solution)/shard_map/ppermute | solution.py:454
  158.4 17.2 %collective-permute-start.15 = (f32[152,256]{1,0:T(8,128)}, f32[152,256]{1,0:T(8,128)S(1)}, u32[]{:S(2)}, u32[]{:S(2)}) collective-permute-start(f32[152,256]{1,0:T(8,128)} %select_maximum_fusion), channel_id=1, source_target_pairs={{0,32},{16,48},{32,64},{48,80},{64,96},{80,112},{96,0},{112,16},{1... | collective-permute-start | bytes 466952 | tf_op jit(solution)/shard_map/ppermute | solution.py:454
  175.6 15.6 %collective-permute-start.16 = (f32[152,256]{1,0:T(8,128)}, f32[152,256]{1,0:T(8,128)S(1)}, u32[]{:S(2)}, u32[]{:S(2)}) collective-permute-start(f32[152,256]{1,0:T(8,128)} %select_maximum_fusion), channel_id=1, source_target_pairs={{0,48},{16,64},{32,80},{48,96},{64,112},{80,0},{96,16},{112,32},{1... | collective-permute-start | bytes 466952 | tf_op jit(solution)/shard_map/ppermute | solution.py:454
  216.7 14.8 %collective-permute-start.20 = (f32[152,256]{1,0:T(8,128)}, f32[152,256]{1,0:T(8,128)S(1)}, u32[]{:S(2)}, u32[]{:S(2)}) collective-permute-start(f32[152,256]{1,0:T(8,128)} %select_maximum_fusion), channel_id=1, source_target_pairs={{0,112},{16,0},{32,16},{48,32},{64,48},{80,64},{96,80},{112,96},{1... | collective-permute-start | bytes 466952 | tf_op jit(solution)/shard_map/ppermute | solution.py:454
  231.5 13.7 %collective-permute-start.29 = (f32[96,8,128]{2,1,0:T(8,128)S(1)}, f32[96,8,128]{2,1,0:T(8,128)S(1)}, u32[]{:S(2)}, u32[]{:S(2)}) collective-permute-start(f32[96,8,128]{2,1,0:T(8,128)S(1)} %collect_rows.1.rest_0_), channel_id=1, source_target_pairs={{0,32},{16,48},{32,64},{48,80},{64,96},{80,112},{96,0},{112,16},{1... | collective-permute-start | bytes 1179656 | tf_op jit(solution)/shard_map/ppermute | solution.py:454
  232.5 12.7 %collective-permute-start.28 = (f32[96,8,128]{2,1,0:T(8,128)S(1)}, f32[96,8,128]{2,1,0:T(8,128)S(1)}, u32[]{:S(2)}, u32[]{:S(2)}) collective-permute-start(f32[96,8,128]{2,1,0:T(8,128)S(1)} %collect_rows.1.rest_0_), channel_id=1, source_target_pairs={{0,16},{16,32},{32,48},{48,64},{64,80},{80,96},{96,112},{112,0},{1... | collective-permute-start | bytes 1179656 | tf_op jit(solution)/shard_map/ppermute | solution.py:454
  (29 other events, 958.0 us)
Sparse Core Ops, SparseCore 0:
  459.3 53.5 all-gather.1
